TPU v7x, 8 devices: a whole 2x2x1 slice. The times are simulated.
8 devices in a mesh: dp: 1 (over z), sp: 8 (over y, x, core).
Axes of the slice: x: 2, y: 2, z: 1, core: 2. Of those that a mesh axis runs over, the one named last changes fastest.
Arguments:
- hidden_in: bfloat16 [8, 512, 1024], P('dp', 'sp')
- positions: int32 [512], P(('dp', 'sp'))
- grad_y: bfloat16 [8, 512, 1024], P('dp', 'sp')
- w_query: bfloat16 [2, 1024, 16, 64], replicated
- w_key: bfloat16 [2, 1024, 16, 64], replicated
- w_value: bfloat16 [2, 1024, 16, 64], replicated
- w_out: bfloat16 [2, 16, 64, 1024], replicated
- w_up: bfloat16 [2, 1024, 4096], replicated
- w_down: bfloat16 [2, 4096, 1024], replicated
- gain: float32 [2, 1024], replicated
- learn_rate: float32 [], replicated
Outputs:
- output 1: bfloat16 [8, 512, 1024], P('dp', 'sp')
- output 2: bfloat16 [8, 512, 1024], P('dp', 'sp')
- output 3: bfloat16 [2, 1024, 16, 64], P('dp')
- output 4: bfloat16 [2, 1024, 16, 64], P('dp')
- output 5: bfloat16 [2, 1024, 16, 64], P('dp')
- output 6: bfloat16 [2, 16, 64, 1024], P('dp')
- output 7: bfloat16 [2, 1024, 4096], P('dp')
- output 8: bfloat16 [2, 4096, 1024], P('dp')
All inputs are finite; a program needn't handle non-finite values.
Results may differ from a plain program's by a relative error of at most 0.0114389.
Values are sent between devices in bfloat16 or wider.
A program may use at most 1 GiB of HBM per device.

v0:
```python
import functools
import jax
import jax.numpy as jnp
from jax import lax
from jax.sharding import PartitionSpec as P

EPSILON = 1e-6
ROPE_BASE = 10000.0
NEG_LARGE = -1e30
gelu_tanh = functools.partial(jax.nn.gelu, approximate=True)


def rope_tables(positions, head_dim):
    half_dim = head_dim // 2
    freqs = ROPE_BASE ** (-jnp.arange(half_dim, dtype=jnp.float32) / half_dim)
    angles = positions.astype(jnp.float32)[:, None] * freqs[None, :]
    return jnp.cos(angles)[None, :, None, :], jnp.sin(angles)[None, :, None, :]


def rotate(tensor, cos_t, sin_t):
    half_dim = tensor.shape[-1] // 2
    first = tensor[..., :half_dim]
    second = tensor[..., half_dim:]
    return jnp.concatenate([first * cos_t - second * sin_t, second * cos_t + first * sin_t], axis=-1)


def norm_apply(x_f32, gain_row):
    inv_rms = lax.rsqrt(jnp.mean(x_f32 * x_f32, axis=-1, keepdims=True) + EPSILON)
    return x_f32 * inv_rms * gain_row


def attn_scores(q_grouped, k_heads, q_offset):
    scale = q_grouped.shape[-1] ** -0.5
    scores = jnp.einsum("bqkgd,bskd->bkgqs", q_grouped, k_heads, preferred_element_type=jnp.float32) * scale
    allowed = (jnp.arange(q_grouped.shape[1])[:, None] + q_offset) >= jnp.arange(k_heads.shape[1])[None, :]
    return jnp.where(allowed, scores, NEG_LARGE)


def attn_forward(q_heads, k_heads, v_heads, q_offset):
    batch, q_len, query_count, head_dim = q_heads.shape
    kv_count = k_heads.shape[2]
    q_grouped = q_heads.reshape(batch, q_len, kv_count, query_count // kv_count, head_dim)
    scores = attn_scores(q_grouped, k_heads, q_offset)
    row_max = jnp.max(scores, axis=-1, keepdims=True)
    log_norm = row_max + jnp.log(jnp.sum(jnp.exp(scores - row_max), axis=-1, keepdims=True))
    probs = jnp.exp(scores - log_norm).astype(jnp.bfloat16)
    attended = jnp.einsum("bkgqs,bskd->bqkgd", probs, v_heads, preferred_element_type=jnp.float32)
    return attended.astype(jnp.bfloat16).reshape(batch, q_len, query_count, head_dim), log_norm


def attn_backward(q_heads, k_heads, v_heads, d_out, log_norm, q_offset):
    batch, q_len, query_count, head_dim = q_heads.shape
    kv_count = k_heads.shape[2]
    q_grouped = q_heads.reshape(batch, q_len, kv_count, query_count // kv_count, head_dim)
    d_grouped = d_out.reshape(batch, q_len, kv_count, query_count // kv_count, head_dim)
    probs = jnp.exp(attn_scores(q_grouped, k_heads, q_offset) - log_norm)
    d_value = jnp.einsum("bkgqs,bqkgd->bskd", probs.astype(jnp.bfloat16), d_grouped, preferred_element_type=jnp.float32)
    d_probs = jnp.einsum("bqkgd,bskd->bkgqs", d_grouped, v_heads, preferred_element_type=jnp.float32)
    row_dot = jnp.sum(d_probs * probs, axis=-1, keepdims=True)
    d_scores = (probs * (d_probs - row_dot) * head_dim ** -0.5).astype(jnp.bfloat16)
    d_query = jnp.einsum("bkgqs,bskd->bqkgd", d_scores, k_heads, preferred_element_type=jnp.float32)
    d_key = jnp.einsum("bkgqs,bqkgd->bskd", d_scores, q_grouped, preferred_element_type=jnp.float32)
    return d_query.reshape(batch, q_len, query_count, head_dim), d_key, d_value


def to_heads(tensor):
    return lax.all_to_all(tensor, "sp", 2, 1, tiled=True)


def to_seq(tensor):
    return lax.all_to_all(tensor, "sp", 1, 2, tiled=True)


def solution(mesh):
    act_spec = P("dp", "sp", None)
    out_four = P("dp", None, None, None)
    out_three = P("dp", None, None)

    def step(hidden_in, positions, grad_y, w_query, w_key, w_value, w_out, w_up, w_down, gain, learn_rate):
        layers = w_query.shape[0]
        cos_t, sin_t = rope_tables(positions, w_query.shape[3])

        def apply_update(weight, local_grad):
            total_grad = lax.psum(local_grad, "sp")
            return (weight.astype(jnp.float32) - learn_rate * total_grad).astype(jnp.bfloat16)

        saved = []
        hidden = hidden_in
        for layer in range(layers):
            x_f32 = hidden.astype(jnp.float32)
            normed = norm_apply(x_f32, gain[layer]).astype(jnp.bfloat16)
            q_seq = rotate(jnp.einsum("bsd,dhe->bshe", normed, w_query[layer], preferred_element_type=jnp.float32), cos_t, sin_t).astype(jnp.bfloat16)
            k_seq = rotate(jnp.einsum("bsd,dhe->bshe", normed, w_key[layer], preferred_element_type=jnp.float32), cos_t, sin_t).astype(jnp.bfloat16)
            v_seq = jnp.einsum("bsd,dhe->bshe", normed, w_value[layer], preferred_element_type=jnp.float32).astype(jnp.bfloat16)
            q_heads = to_heads(q_seq)
            k_heads = to_heads(k_seq)
            v_heads = to_heads(v_seq)
            o_heads, log_norm = attn_forward(q_heads, k_heads, v_heads, 0)
            o_seq = to_seq(o_heads)
            attn_part = jnp.einsum("bshe,hed->bsd", o_seq, w_out[layer], preferred_element_type=jnp.float32)
            pre_act = jnp.einsum("bsd,df->bsf", normed, w_up[layer], preferred_element_type=jnp.float32)
            act_out = gelu_tanh(pre_act).astype(jnp.bfloat16)
            mlp_part = jnp.einsum("bsf,fd->bsd", act_out, w_down[layer], preferred_element_type=jnp.float32)
            saved.append((hidden, normed, q_heads, k_heads, v_heads, o_seq, log_norm, pre_act, act_out))
            hidden = (x_f32 + attn_part + mlp_part).astype(jnp.bfloat16)
        out_y = hidden

        new_query = [None] * layers
        new_key = [None] * layers
        new_value = [None] * layers
        new_out = [None] * layers
        new_up = [None] * layers
        new_down = [None] * layers
        grad_h = grad_y
        for layer in reversed(range(layers)):
            hidden_prev, normed, q_heads, k_heads, v_heads, o_seq, log_norm, pre_act, act_out = saved[layer]
            d_act = jnp.einsum("bsd,fd->bsf", grad_h, w_down[layer], preferred_element_type=jnp.float32).astype(jnp.bfloat16)
            d_pre = jax.vjp(gelu_tanh, pre_act)[1](d_act.astype(jnp.float32))[0].astype(jnp.bfloat16)
            d_o_seq = jnp.einsum("bsd,hed->bshe", grad_h, w_out[layer], preferred_element_type=jnp.float32).astype(jnp.bfloat16)
            d_o_heads = to_heads(d_o_seq)
            dq_heads, dk_heads, dv_heads = attn_backward(q_heads, k_heads, v_heads, d_o_heads, log_norm, 0)
            d_q_seq = to_seq(dq_heads.astype(jnp.bfloat16))
            d_k_seq = to_seq(dk_heads.astype(jnp.bfloat16))
            d_v_seq = to_seq(dv_heads.astype(jnp.bfloat16))
            d_q_pre = rotate(d_q_seq.astype(jnp.float32), cos_t, -sin_t).astype(jnp.bfloat16)
            d_k_pre = rotate(d_k_seq.astype(jnp.float32), cos_t, -sin_t).astype(jnp.bfloat16)
            d_normed = (jnp.einsum("bshe,dhe->bsd", d_q_pre, w_query[layer], preferred_element_type=jnp.float32)
                        + jnp.einsum("bshe,dhe->bsd", d_k_pre, w_key[layer], preferred_element_type=jnp.float32)
                        + jnp.einsum("bshe,dhe->bsd", d_v_seq, w_value[layer], preferred_element_type=jnp.float32)
                        + jnp.einsum("bsf,df->bsd", d_pre, w_up[layer], preferred_element_type=jnp.float32))
            norm_fn = functools.partial(norm_apply, gain_row=gain[layer])
            d_norm_in = jax.vjp(norm_fn, hidden_prev.astype(jnp.float32))[1](d_normed)[0]
            new_down[layer] = apply_update(w_down[layer], jnp.einsum("bsf,bsd->fd", act_out, grad_h, preferred_element_type=jnp.float32))
            new_up[layer] = apply_update(w_up[layer], jnp.einsum("bsd,bsf->df", normed, d_pre, preferred_element_type=jnp.float32))
            new_out[layer] = apply_update(w_out[layer], jnp.einsum("bshe,bsd->hed", o_seq, grad_h, preferred_element_type=jnp.float32))
            new_query[layer] = apply_update(w_query[layer], jnp.einsum("bsd,bshe->dhe", normed, d_q_pre, preferred_element_type=jnp.float32))
            new_key[layer] = apply_update(w_key[layer], jnp.einsum("bsd,bshe->dhe", normed, d_k_pre, preferred_element_type=jnp.float32))
            new_value[layer] = apply_update(w_value[layer], jnp.einsum("bsd,bshe->dhe", normed, d_v_seq, preferred_element_type=jnp.float32))
            grad_h = (grad_h.astype(jnp.float32) + d_norm_in).astype(jnp.bfloat16)
        return (out_y, grad_h, jnp.stack(new_query), jnp.stack(new_key), jnp.stack(new_value), jnp.stack(new_out), jnp.stack(new_up), jnp.stack(new_down))

    return jax.shard_map(step, mesh=mesh,
                         in_specs=(act_spec, P(("dp", "sp")), act_spec, P(), P(), P(), P(), P(), P(), P(), P()),
                         out_specs=(act_spec, act_spec, out_four, out_four, out_four, out_four, out_three, out_three),
                         check_vma=False)
```

profile of v0, /device:TPU:1, one launch (start us, length us, event | category | flops | bytes accessed | tf_op | source)
XLA Modules:
  0.0 1876.7 jit_solution(15266504439247738161)
XLA Ops:
  32.5 7.0 all-to-all-done.1
  39.5 7.2 all-to-all-start.2
  85.9 7.7 fusion.248
  93.6 8.3 exponential_reduce_fusion.1
  114.1 8.8 fusion.191
  134.3 10.2 fusion.52
  162.4 11.9 fusion.90
  183.6 7.0 fusion.44
  196.5 15.4 convolution_bitcast_fusion
  223.2 14.1 fusion.12
  243.5 12.9 convolution_bitcast_fusion.2
  288.2 7.7 fusion.249
  295.9 8.2 exponential_reduce_fusion
  304.1 9.4 fusion.194
  327.3 11.3 fusion.4
  338.6 12.0 fusion.36
  368.0 10.5 fusion.42
  395.0 8.4 fusion.197
  456.5 12.3 fusion.17
  473.0 15.0 convolution_bitcast_fusion.1
  496.9 10.5 convolution_bitcast_fusion.3
  508.4 7.2 all-to-all-start.7
  528.1 11.6 fusion
  539.7 12.1 fusion.37
  609.1 9.5 fusion.188
  683.2 10.6 fusion.50
  693.9 10.7 fusion.94
  717.0 1073.6 %all-reduce.3.cloned.1.call-done = (f32[1024,16,64]{0,2,1:T(8,128)}, f32[1024,16,64]{0,2,1:T(8,128)}, f32[1024,16,64]{0,2,1:T(8,128)}, f32[1024,16,64]{0,2,1:T(8...) async-done(((f32[1024,16,64]{0,2,1:T(8,128)}, ...) | async-done | bytes 100663312 | tf_op jit(solution)/shard_map/psum | solution.py:84
  1822.0 17.0 fusion.32
  1839.0 6.8 pad_maximum_fusion
  1845.7 17.2 fusion.34
  1862.9 6.8 pad_maximum_fusion.1
  (331 shorter events, 461.5 us)
Async XLA Ops:
  8.0 126.4 %copy-start.62 = (f32[1,1024]{1,0:T(1,128)}, f32[1,1024]{1,0:T(1,128)S(1)}, u32[]{:S(2)}) copy-start(f32[1,1024]{1,0:T(1,128)S(1)} %get-tuple-element.57) | copy-start | bytes 12292
  9.5 124.8 %copy-start.68 = (f32[8,64]{1,0:T(8,128)}, f32[8,64]{1,0:T(8,128)S(1)}, u32[]{:S(2)}) copy-start(f32[8,64]{1,0:T(8,128)S(1)} %fusion.221) | copy-start | bytes 6148
  17.9 421.9 %copy-start.60 = (f32[64,32]{0,1:T(8,128)}, f32[64,32]{0,1:T(8,128)S(1)}, u32[]{:S(2)}) copy-start(f32[64,32]{0,1:T(8,128)S(1)} %get-tuple-element.60) | copy-start | bytes 24580
  24.0 15.5 all-to-all-start.1
  39.5 31.0 %all-to-all-start.2 = ((bf16[8,2,32768]{2,1,0:T(2,128)(2,1)}), bf16[8,2,32768]{2,1,0:T(2,128)(2,1)}, u32[]{:S(2)}, u32[]{:S(2)}) async-start(bf16[8,2,32768]{2,1,0:T(2,128)(2,1)} %reshape.332), calls=%async_computation.2 | async-start | bytes 2097152 | tf_op jit(solution)/shard_map/all_to_all | solution.py:67
  70.5 15.4 copy-start.9
  70.5 31.4 %all-to-all-start = ((bf16[8,2,32768]{2,1,0:T(2,128)(2,1)}), bf16[8,2,32768]{2,1,0:T(2,128)(2,1)}, u32[]{:S(2)}, u32[]{:S(2)}) async-start(bf16[8,2,32768]{2,1,0:T(2,128)(2,1)} %reshape.328), calls=%async_computation | async-start | bytes 2097152 | tf_op jit(solution)/shard_map/all_to_all | solution.py:67
  101.9 29.1 %all-to-all-start.8 = ((bf16[8,2,32768]{2,1,0:T(2,128)(2,1)}), bf16[8,2,32768]{2,1,0:T(2,128)(2,1)}, u32[]{:S(2)}, u32[]{:S(2)}) async-start(bf16[8,2,32768]{2,1,0:T(2,128)(2,1)} %reshape.344), calls=%async_computation.8 | async-start | bytes 2097152 | tf_op jit(solution)/shard_map/all_to_all | solution.py:67
  131.1 22.6 %all-to-all-start.3 = ((bf16[8,2,32768]{2,1,0:T(2,128)(2,1)}), bf16[8,2,32768]{2,1,0:T(2,128)(2,1)}, u32[]{:S(2)}, u32[]{:S(2)}) async-start(bf16[8,2,32768]{2,1,0:T(2,128)(2,1)} %reshape.334), calls=%async_computation.3 | async-start | bytes 2097152 | tf_op jit(solution)/shard_map/all_to_all | solution.py:71
  162.4 21.2 %slice-start = ((s8[16777216]{0:T(1024)(128)(4,1)}), s8[4194304]{0:T(1024)(128)(4,1)S(1)}, s32[]{:S(2)}) async-start(s8[16777216]{0:T(1024)(128)(4,1)} %bitcast.554), calls=%async_computation.17 | async-start | bytes 8388608
  162.4 21.2 %slice-start.1 = ((s8[16777216]{0:T(1024)(128)(4,1)}), s8[4194304]{0:T(1024)(128)(4,1)S(1)}, s32[]{:S(2)}) async-start(s8[16777216]{0:T(1024)(128)(4,1)} %bitcast.554), calls=%async_computation.18 | async-start | bytes 8388608
  162.4 21.2 %slice-start.2 = ((s8[16777216]{0:T(1024)(128)(4,1)}), s8[4194304]{0:T(1024)(128)(4,1)S(1)}, s32[]{:S(2)}) async-start(s8[16777216]{0:T(1024)(128)(4,1)} %bitcast.554), calls=%async_computation.19 | async-start | bytes 8388608
  193.5 26.5 %all-to-all-start.4 = ((bf16[8,2,32768]{2,1,0:T(2,128)(2,1)}), bf16[8,2,32768]{2,1,0:T(2,128)(2,1)}, u32[]{:S(2)}, u32[]{:S(2)}) async-start(bf16[8,2,32768]{2,1,0:T(2,128)(2,1)} %reshape.336), calls=%async_computation.4 | async-start | bytes 2097152 | tf_op jit(solution)/shard_map/all_to_all | solution.py:67
  196.5 15.4 copy-start.3
  196.5 15.4 copy-start.39
  220.0 20.5 %all-to-all-start.5 = ((bf16[8,2,32768]{2,1,0:T(2,128)(2,1)}), bf16[8,2,32768]{2,1,0:T(2,128)(2,1)}, u32[]{:S(2)}, u32[]{:S(2)}) async-start(bf16[8,2,32768]{2,1,0:T(2,128)(2,1)} %reshape.338), calls=%async_computation.5 | async-start | bytes 2097152 | tf_op jit(solution)/shard_map/all_to_all | solution.py:67
  240.5 35.3 %all-to-all-start.6 = ((bf16[8,2,32768]{2,1,0:T(2,128)(2,1)}), bf16[8,2,32768]{2,1,0:T(2,128)(2,1)}, u32[]{:S(2)}, u32[]{:S(2)}) async-start(bf16[8,2,32768]{2,1,0:T(2,128)(2,1)} %reshape.340), calls=%async_computation.6 | async-start | bytes 2097152 | tf_op jit(solution)/shard_map/all_to_all | solution.py:67
  323.8 41.2 %all-to-all-start.11 = ((bf16[8,2,32768]{2,1,0:T(2,128)(2,1)}), bf16[8,2,32768]{2,1,0:T(2,128)(2,1)}, u32[]{:S(2)}, u32[]{:S(2)}) async-start(bf16[8,2,32768]{2,1,0:T(2,128)(2,1)} %reshape.346), calls=%async_computation.11 | async-start | bytes 2097152 | tf_op jit(solution)/shard_map/all_to_all | solution.py:71
  365.0 26.8 %all-to-all-start.10 = ((bf16[8,2,32768]{2,1,0:T(2,128)(2,1)}), bf16[8,2,32768]{2,1,0:T(2,128)(2,1)}, u32[]{:S(2)}, u32[]{:S(2)}) async-start(bf16[8,2,32768]{2,1,0:T(2,128)(2,1)} %reshape.350), calls=%async_computation.10 | async-start | bytes 2097152 | tf_op jit(solution)/shard_map/all_to_all | solution.py:71
  391.8 37.1 %all-to-all-start.9 = ((bf16[8,2,32768]{2,1,0:T(2,128)(2,1)}), bf16[8,2,32768]{2,1,0:T(2,128)(2,1)}, u32[]{:S(2)}, u32[]{:S(2)}) async-start(bf16[8,2,32768]{2,1,0:T(2,128)(2,1)} %reshape.348), calls=%async_computation.9 | async-start | bytes 2097152 | tf_op jit(solution)/shard_map/all_to_all | solution.py:71
  439.8 16.6 slice-start.4
  439.8 16.6 slice-start.5
  456.5 16.5 copy-start.15
  493.9 14.5 all-to-all-start.12
  508.4 60.8 %all-to-all-start.7 = ((bf16[8,2,32768]{2,1,0:T(2,128)(2,1)}), bf16[8,2,32768]{2,1,0:T(2,128)(2,1)}, u32[]{:S(2)}, u32[]{:S(2)}) async-start(bf16[8,2,32768]{2,1,0:T(2,128)(2,1)} %reshape.342), calls=%async_computation.7 | async-start | bytes 2097152 | tf_op jit(solution)/shard_map/all_to_all | solution.py:71
  539.7 15.6 copy-start.12
  569.2 23.9 %all-to-all-start.14 = ((bf16[8,2,32768]{2,1,0:T(2,128)(2,1)}), bf16[8,2,32768]{2,1,0:T(2,128)(2,1)}, u32[]{:S(2)}, u32[]{:S(2)}) async-start(bf16[8,2,32768]{2,1,0:T(2,128)(2,1)} %reshape.358), calls=%async_computation.14 | async-start | bytes 2097152 | tf_op jit(solution)/shard_map/all_to_all | solution.py:71
  593.1 35.7 %all-to-all-start.13 = ((bf16[8,2,32768]{2,1,0:T(2,128)(2,1)}), bf16[8,2,32768]{2,1,0:T(2,128)(2,1)}, u32[]{:S(2)}, u32[]{:S(2)}) async-start(bf16[8,2,32768]{2,1,0:T(2,128)(2,1)} %reshape.356), calls=%async_computation.13 | async-start | bytes 2097152 | tf_op jit(solution)/shard_map/all_to_all | solution.py:71
  628.9 32.0 %all-to-all-start.15 = ((bf16[8,2,32768]{2,1,0:T(2,128)(2,1)}), bf16[8,2,32768]{2,1,0:T(2,128)(2,1)}, u32[]{:S(2)}, u32[]{:S(2)}) async-start(bf16[8,2,32768]{2,1,0:T(2,128)(2,1)} %reshape.354), calls=%async_computation.15 | async-start | bytes 2097152 | tf_op jit(solution)/shard_map/all_to_all | solution.py:71
  631.8 1158.8 %all-reduce.3.cloned.1.call-start = ((), (), s32[]{:S(2)}) async-start(), calls=%async_computation.16 | async-start | bytes 201326592 | tf_op jit(solution)/shard_map/psum | solution.py:84
  678.2 15.7 slice-start.8
  678.2 15.7 slice-start.9
  (69 other events, 417.9 us)
Sparse Core Ops, SparseCore 0:
  677.6 1112.9 all-reduce.2
where the time goes:
time: 1890 us; the launch traced here: 1880 us
  waiting for transfers between devices  1080 us (57%)
  matrix products  326 us (17%)
  local copies, waits for them, and re-layouts  263 us (14%)
  other arithmetic  132 us (7%)
  starting transfers between devices  58.5 us (3%)
    psum x1, waiting for transfers between devices, apply_update(): total_grad = lax.psum(local_grad, 'sp')  1070 us
    unnamed x200, local copies, waits for them, and re-layouts  132 us
    all_to_all x12, local copies, waits for them, and re-layouts, to_heads(): return lax.all_to_all(tensor, 'sp', 2, 1, tiled=True)  41.9 us
  transfers between devices with their start and end apart: 17, of which 3 were waited for; matrix products, arithmetic and copies ran while one was open for 23% of the time, Pallas kernels for 0%

commit v1 on v0

v1 whole, which is shorter than its diff:
```python
import functools
import jax
import jax.numpy as jnp
from jax import lax
from jax.experimental import pallas as pl
from jax.experimental.pallas import tpu as pltpu
from jax.sharding import PartitionSpec as P

EPSILON = 1e-6
ROPE_BASE = 10000.0
NEG_LARGE = -1e30
HD = 64
SEQ = 512
D = 1024
CB = 256
QB = 256
BF = jnp.bfloat16
F32 = jnp.float32


def norm_apply(x_f32, gain_row):
    inv_rms = lax.rsqrt(jnp.mean(x_f32 * x_f32, axis=-1, keepdims=True) + EPSILON)
    return x_f32 * inv_rms * gain_row


def dot_nn(a, b):
    return lax.dot_general(a, b, (((1,), (0,)), ((), ())), preferred_element_type=F32)


def dot_nt(a, b):
    return lax.dot_general(a, b, (((1,), (1,)), ((), ())), preferred_element_type=F32)


def swap_halves(t):
    lane = lax.broadcasted_iota(jnp.int32, t.shape, 1)
    return jnp.where(lane % HD < HD // 2, pltpu.roll(t, t.shape[1] - HD // 2, 1), pltpu.roll(t, HD // 2, 1))


def head_mask(rows, h):
    lane = lax.broadcasted_iota(jnp.int32, (rows, 128), 1)
    return lane < HD if h % 2 == 0 else lane >= HD


def causal_mask(nk, j):
    key = lax.broadcasted_iota(jnp.int32, (nk, QB), 0)
    qry = lax.broadcasted_iota(jnp.int32, (nk, QB), 1) + j * QB
    return key <= qry


def attn_fwd_kernel(n_ref, wq_ref, wk_ref, wv_ref, c_ref, s_ref, q_ref, k_ref, v_ref, o_ref, op_ref, lse_ref):
    n = n_ref[...]
    c = jnp.concatenate([c_ref[...]] * (CB // 128), axis=1)
    s = jnp.concatenate([s_ref[...]] * (CB // 128), axis=1)
    qf = dot_nn(n, wq_ref[...])
    q = (qf * c + swap_halves(qf) * s).astype(BF)
    kf = dot_nn(n, wk_ref[...])
    k = (kf * c + swap_halves(kf) * s).astype(BF)
    v = dot_nn(n, wv_ref[...]).astype(BF)
    q_ref[...] = q
    k_ref[...] = k
    v_ref[...] = v
    vt = v.T
    heads = []
    for h in range(CB // HD):
        lo = (h // 2) * 128
        qm = jnp.where(head_mask(SEQ, h), q[:, lo:lo + 128] * BF(HD ** -0.5), BF(0))
        k2 = k[:, lo:lo + 128]
        cols = []
        for j in range(SEQ // QB):
            nk = (j + 1) * QB
            st = dot_nt(k2[:nk], qm[j * QB:(j + 1) * QB])
            st = jnp.where(causal_mask(nk, j), st, NEG_LARGE)
            m = jnp.max(st, axis=0, keepdims=True)
            e = jnp.exp(st - m)
            l = jnp.sum(e, axis=0, keepdims=True)
            p = (e * (1.0 / l)).astype(BF)
            cols.append(dot_nn(vt[h * HD:(h + 1) * HD, :nk], p))
            lse_ref[h:h + 1, j * QB:(j + 1) * QB] = m + jnp.log(l)
        heads.append(jnp.concatenate(cols, axis=1))
    o = jnp.concatenate(heads, axis=0).T.astype(BF)
    o_ref[...] = o
    op_ref[0] = o[:, :128]
    op_ref[1] = o[:, 128:]


def attn_fwd(l, n, wq, wk, wv, c, s):
    nb = D // CB
    wspec = pl.BlockSpec((None, D, CB), lambda i: (l, 0, i))
    aspec = pl.BlockSpec((SEQ, CB), lambda i: (0, i))
    full = lambda shape: pl.BlockSpec(shape, lambda i: (0, 0))
    act = jax.ShapeDtypeStruct((SEQ, D), BF)
    return pl.pallas_call(
        attn_fwd_kernel,
        grid=(nb,),
        in_specs=[full((SEQ, D)), wspec, wspec, wspec, full((SEQ, 128)), full((SEQ, 128))],
        out_specs=[aspec, aspec, aspec, aspec, pl.BlockSpec((2, SEQ, 128), lambda i: (i, 0, 0)),
                   pl.BlockSpec((None, CB // HD, SEQ), lambda i: (i, 0, 0))],
        out_shape=[act, act, act, act, jax.ShapeDtypeStruct((8, SEQ, 128), BF),
                   jax.ShapeDtypeStruct((nb, CB // HD, SEQ), F32)],
        cost_estimate=pl.CostEstimate(flops=6 * SEQ * D * D + 8 * SEQ * SEQ * D, bytes_accessed=14 << 20, transcendentals=0),
        name="attn_fwd",
    )(n, wq, wk, wv, c, s)


def attn_bwd_kernel(g_ref, wo_ref, wq_ref, wk_ref, wv_ref, q_ref, k_ref, v_ref, lse_ref, c_ref, s_ref, dn_ref, dp_ref):
    do = dot_nt(g_ref[...], wo_ref[...]).astype(BF)
    q = q_ref[...]
    k = k_ref[...]
    v = v_ref[...]
    kt = k.T
    dqs, dks, dvs = [], [], []
    for h in range(CB // HD):
        lo = (h // 2) * 128
        hm = head_mask(SEQ, h)
        q2 = q[:, lo:lo + 128]
        qm = jnp.where(hm, q2 * BF(HD ** -0.5), BF(0))
        do2 = do[:, lo:lo + 128]
        dom = jnp.where(hm, do2, BF(0))
        k2 = k[:, lo:lo + 128]
        v2 = v[:, lo:lo + 128]
        dk = dv = None
        cols = []
        for j in reversed(range(SEQ // QB)):
            nk = (j + 1) * QB
            rows = slice(j * QB, (j + 1) * QB)
            st = dot_nt(k2[:nk], qm[rows])
            pt = jnp.where(causal_mask(nk, j), jnp.exp(st - lse_ref[h:h + 1, rows]), 0.0)
            dpt = dot_nt(v2[:nk], dom[rows])
            rd = jnp.sum(dpt * pt, axis=0, keepdims=True)
            dst = (pt * (dpt - rd) * HD ** -0.5).astype(BF)
            dv_j = dot_nn(pt.astype(BF), do2[rows])
            dk_j = dot_nn(dst, q2[rows])
            cols.append(dot_nn(kt[h * HD:(h + 1) * HD, :nk], dst))
            if dk is None:
                dk, dv = dk_j, dv_j
            else:
                dk = jnp.concatenate([dk[:nk] + dk_j, dk[nk:]], axis=0)
                dv = jnp.concatenate([dv[:nk] + dv_j, dv[nk:]], axis=0)
        dqs.append(jnp.concatenate(cols[::-1], axis=1))
        dks.append(dk)
        dvs.append(dv)
    c = jnp.concatenate([c_ref[...]] * (CB // 128), axis=1)
    s = jnp.concatenate([s_ref[...]] * (CB // 128), axis=1)
    low = head_mask(SEQ, 0)

    def join(parts):
        return jnp.concatenate([jnp.where(low, parts[2 * i], parts[2 * i + 1]) for i in range(CB // 128)], axis=1).astype(BF)

    def unrope(t):
        t = t.astype(F32)
        return (t * c - swap_halves(t) * s).astype(BF)

    dq = unrope(jnp.concatenate(dqs, axis=0).T.astype(BF))
    dk = unrope(join(dks))
    dv = join(dvs)
    for i in range(2):
        dp_ref[i, :, 0:128] = dq[:, i * 128:(i + 1) * 128]
        dp_ref[i, :, 128:256] = dk[:, i * 128:(i + 1) * 128]
        dp_ref[i, :, 256:384] = dv[:, i * 128:(i + 1) * 128]
    dn = dot_nt(dq, wq_ref[...]) + dot_nt(dk, wk_ref[...]) + dot_nt(dv, wv_ref[...])

    @pl.when(pl.program_id(0) == 0)
    def _():
        dn_ref[...] = dn

    @pl.when(pl.program_id(0) > 0)
    def _():
        dn_ref[...] += dn


def attn_bwd(l, g, wo, wq, wk, wv, q, k, v, lse, c, s):
    nb = D // CB
    wspec = pl.BlockSpec((None, D, CB), lambda i: (l, 0, i))
    aspec = pl.BlockSpec((SEQ, CB), lambda i: (0, i))
    full = lambda shape: pl.BlockSpec(shape, lambda i: (0, 0))
    return pl.pallas_call(
        attn_bwd_kernel,
        grid=(nb,),
        in_specs=[full((SEQ, D)), pl.BlockSpec((None, CB, D), lambda i: (l, i, 0)), wspec, wspec, wspec, aspec, aspec, aspec,
                  pl.BlockSpec((None, CB // HD, SEQ), lambda i: (i, 0, 0)), full((SEQ, 128)), full((SEQ, 128))],
        out_specs=[full((SEQ, D)), pl.BlockSpec((2, SEQ, 384), lambda i: (i, 0, 0))],
        out_shape=[jax.ShapeDtypeStruct((SEQ, D), F32), jax.ShapeDtypeStruct((8, SEQ, 384), BF)],
        cost_estimate=pl.CostEstimate(flops=8 * SEQ * D * D + 20 * SEQ * SEQ * D, bytes_accessed=20 << 20, transcendentals=0),
        name="attn_bwd",
    )(g, wo, wq, wk, wv, q, k, v, lse, c, s)


NDEV = 8
MESH_ID = pl.DeviceIdType.MESH
ANY = pl.BlockSpec(memory_space=pl.ANY)
FB = 512


class Exchange:
    def __init__(self, pairs, send_sem, recv_sem, local_sem):
        me = lax.axis_index("sp")
        self.remote, self.local = [], []
        for a, (src, dst) in enumerate(pairs):
            self.local.append(pltpu.make_async_copy(src.at[me], dst.at[me], local_sem.at[a]))
        for k in range(1, NDEV):
            peer = lax.rem(me + k, NDEV)
            for a, (src, dst) in enumerate(pairs):
                self.remote.append(pltpu.make_async_remote_copy(
                    src_ref=src.at[peer], dst_ref=dst.at[me], send_sem=send_sem.at[a, k], recv_sem=recv_sem.at[a, k],
                    device_id={"sp": peer}, device_id_type=MESH_ID))

    def start(self):
        me = lax.axis_index("sp")
        barrier = pltpu.get_barrier_semaphore()
        for k in range(1, NDEV):
            pl.semaphore_signal(barrier, inc=1, device_id={"sp": lax.rem(me + k, NDEV)}, device_id_type=MESH_ID)
        for c in self.local:
            c.start()
        pl.semaphore_wait(barrier, NDEV - 1)
        for c in self.remote:
            c.start()

    def wait(self):
        for c in self.local + self.remote:
            c.wait()


def exchange_sems(n):
    return [pltpu.SemaphoreType.DMA((n, NDEV)), pltpu.SemaphoreType.DMA((n, NDEV)), pltpu.SemaphoreType.DMA((n,))]


def entry_kernel(x_ref, p_ref, xo_ref, po_ref, ss, rs, ls):
    ex = Exchange([(x_ref, xo_ref), (p_ref, po_ref)], ss, rs, ls)
    ex.start()
    ex.wait()


def entry(x, pos):
    return pl.pallas_call(
        entry_kernel, in_specs=[ANY, ANY], out_specs=[ANY, ANY],
        out_shape=[jax.ShapeDtypeStruct(x.shape, x.dtype), jax.ShapeDtypeStruct(pos.shape, pos.dtype)],
        scratch_shapes=exchange_sems(2),
        compiler_params=pltpu.CompilerParams(collective_id=1, has_side_effects=True), name="entry",
    )(x, pos)


def gelu_parts(x):
    c = 0.7978845608028654
    x2 = x * x
    t = jnp.tanh(c * (x + 0.044715 * (x2 * x)))
    return x2, t, c


def gelu(x):
    _, t, _ = gelu_parts(x)
    return x * (0.5 * (1.0 + t))


def gelu_slope(x):
    x2, t, c = gelu_parts(x)
    return 0.5 * (1.0 + t) + 0.5 * x * (1.0 - t * t) * (c * (1.0 + 3 * 0.044715 * x2))


def mlp_fwd_kernel(last, n_ref, x_ref, o_ref, wo_ref, wu_ref, wd_ref, gain_ref, op_ref, *rest):
    if last:
        pre_ref, h_ref, oa_ref, acc_ref, ss, rs, ls = rest
    else:
        pre_ref, h_ref, oa_ref, nn_ref, acc_ref, ss, rs, ls = rest
    i = pl.program_id(0)
    ex = Exchange([(op_ref, oa_ref)], ss, rs, ls)

    @pl.when(i == 0)
    def _():
        ex.start()
        acc_ref[...] = x_ref[...].astype(F32) + dot_nn(o_ref[...], wo_ref[...])

    pre = dot_nn(n_ref[...], wu_ref[...])
    pre_ref[...] = pre
    acc_ref[...] += dot_nn(gelu(pre).astype(BF), wd_ref[...])

    @pl.when(i == pl.num_programs(0) - 1)
    def _():
        h = acc_ref[...].astype(BF)
        h_ref[...] = h
        if not last:
            nn_ref[...] = norm_apply(h.astype(F32), gain_ref[...]).astype(BF)
        ex.wait()


def mlp_fwd(l, last, n, x, o, wo, wu, wd, gain_next, o_pack):
    full = lambda shape: pl.BlockSpec(shape, lambda i: (0, 0))
    ff = wu.shape[2]
    act = jax.ShapeDtypeStruct((SEQ, D), BF)
    out_specs = [pl.BlockSpec((SEQ, FB), lambda i: (0, i)), full((SEQ, D)), ANY]
    out_shape = [jax.ShapeDtypeStruct((SEQ, ff), F32), act, jax.ShapeDtypeStruct(o_pack.shape, BF)]
    if not last:
        out_specs.append(full((SEQ, D)))
        out_shape.append(act)
    return pl.pallas_call(
        functools.partial(mlp_fwd_kernel, last), grid=(ff // FB,),
        in_specs=[full((SEQ, D)), full((SEQ, D)), full((SEQ, D)), pl.BlockSpec((None, D, D), lambda i: (l, 0, 0)),
                  pl.BlockSpec((None, D, FB), lambda i: (l, 0, i)), pl.BlockSpec((None, FB, D), lambda i: (l, i, 0)),
                  full((1, D)), ANY],
        out_specs=out_specs, out_shape=out_shape,
        scratch_shapes=[pltpu.VMEM((SEQ, D), F32)] + exchange_sems(1),
        compiler_params=pltpu.CompilerParams(collective_id=2 + l, has_side_effects=True),
        cost_estimate=pl.CostEstimate(flops=4 * SEQ * D * ff + 2 * SEQ * D * D, bytes_accessed=30 << 20, transcendentals=0),
        name="mlp_fwd",
    )(n, x, o, wo, wu, wd, gain_next, o_pack)


def mlp_bwd_kernel(g_ref, pre_ref, wu_ref, wd_ref, dn_ref, x_ref, gain_ref, go_ref, acc_ref):
    i = pl.program_id(0)

    @pl.when(i == 0)
    def _():
        acc_ref[...] = dn_ref[...]

    d_act = dot_nt(g_ref[...], wd_ref[...]).astype(BF)
    d_pre = (d_act.astype(F32) * gelu_slope(pre_ref[...])).astype(BF)
    acc_ref[...] += dot_nt(d_pre, wu_ref[...])

    @pl.when(i == pl.num_programs(0) - 1)
    def _():
        x = x_ref[...].astype(F32)
        r = lax.rsqrt(jnp.mean(x * x, axis=-1, keepdims=True) + EPSILON)
        t = acc_ref[...] * gain_ref[...]
        dot = jnp.mean(x * t, axis=-1, keepdims=True)
        dx = r * t - x * (r * r * r * dot)
        go_ref[...] = (g_ref[...].astype(F32) + dx).astype(BF)


def mlp_bwd(l, g, pre, wu, wd, dn, x, gain_row):
    full = lambda shape: pl.BlockSpec(shape, lambda i: (0, 0))
    ff = wu.shape[2]
    return pl.pallas_call(
        mlp_bwd_kernel, grid=(ff // FB,),
        in_specs=[full((SEQ, D)), pl.BlockSpec((SEQ, FB), lambda i: (0, i)), pl.BlockSpec((None, D, FB), lambda i: (l, 0, i)),
                  pl.BlockSpec((None, FB, D), lambda i: (l, i, 0)), full((SEQ, D)), full((SEQ, D)), full((1, D))],
        out_specs=full((SEQ, D)), out_shape=jax.ShapeDtypeStruct((SEQ, D), BF),
        scratch_shapes=[pltpu.VMEM((SEQ, D), F32)],
        cost_estimate=pl.CostEstimate(flops=4 * SEQ * D * ff, bytes_accessed=30 << 20, transcendentals=0),
        name="mlp_bwd",
    )(g, pre, wu, wd, dn, x, gain_row)


def dw_mlp_kernel(lr_ref, n_ref, g_ref, wu_ref, wd_ref, dp_ref, sq_ref, w_ref, da_ref, so_ref, wut_ref, au_ref, ad_ref, ss, rs, ls):
    i = pl.program_id(0)
    ex = Exchange([(dp_ref, da_ref), (sq_ref, so_ref)], ss, rs, ls)

    @pl.when(i == 0)
    def _():
        ex.start()
        wut_ref[...] = wu_ref[...].T
        au_ref[...] = jnp.zeros_like(au_ref)
        ad_ref[...] = jnp.zeros_like(ad_ref)

    n = n_ref[...]
    g = g_ref[...].reshape(SEQ, D)
    pre = dot_nt(wut_ref[...], n)
    d_act = dot_nt(wd_ref[...], g).astype(BF)
    x2, t, c = gelu_parts(pre)
    half = 0.5 * (1.0 + t)
    act = (pre * half).astype(BF)
    slope = half + 0.5 * pre * (1.0 - t * t) * (c * (1.0 + 3 * 0.044715 * x2))
    d_pre = (d_act.astype(F32) * slope).astype(BF)
    ad_ref[...] += dot_nn(act, g)
    au_ref[...] += dot_nn(d_pre, n)

    @pl.when(i == pl.num_programs(0) - 1)
    def _():
        lr = lr_ref[0]
        w_ref[0:D] = (wut_ref[...].astype(F32) - lr * au_ref[...]).astype(BF).T
        nd = (wd_ref[...].astype(F32) - lr * ad_ref[...]).astype(BF)
        w_ref[D:D + FB] = nd[:, :FB]
        w_ref[D + FB:] = nd[:, FB:]
        ex.wait()


def dw_mlp(l, lr, n_all, g4, wu_s, wd_s, d_pack, seq_out):
    full = lambda shape: pl.BlockSpec(shape, lambda i: (0, 0))
    gs = g4.shape
    return pl.pallas_call(
        dw_mlp_kernel, grid=(NDEV,),
        in_specs=[pl.BlockSpec(memory_space=pltpu.SMEM), pl.BlockSpec((SEQ, D), lambda i: (i, 0)),
                  pl.BlockSpec((gs[0], None, gs[2], D), lambda i: (0, i, 0, 0)), full((D, FB)), full((FB, D)), ANY, ANY],
        out_specs=[full((2 * D, FB)), ANY, ANY],
        out_shape=[jax.ShapeDtypeStruct((2 * D, FB), BF), jax.ShapeDtypeStruct(d_pack.shape, BF),
                   jax.ShapeDtypeStruct(seq_out.shape, BF)],
        scratch_shapes=[pltpu.VMEM((FB, D), BF), pltpu.VMEM((FB, D), F32), pltpu.VMEM((FB, D), F32)] + exchange_sems(2),
        compiler_params=pltpu.CompilerParams(collective_id=4 + l, has_side_effects=True),
        cost_estimate=pl.CostEstimate(flops=8 * NDEV * SEQ * D * FB, bytes_accessed=24 << 20, transcendentals=0),
        name="dw_mlp",
    )(lr, n_all, g4, wu_s, wd_s, d_pack, seq_out)


def dw_attn_kernel(lr_ref, n_ref, g_ref, d_ref, o_ref, wqkv_ref, wo_ref, w_ref, aq_ref, ao_ref):
    i = pl.program_id(0)

    @pl.when(i == 0)
    def _():
        aq_ref[...] = jnp.zeros_like(aq_ref)
        ao_ref[...] = jnp.zeros_like(ao_ref)

    aq_ref[...] += dot_nn(d_ref[...].T, n_ref[...])
    ao_ref[...] += dot_nn(o_ref[...].T, g_ref[...].reshape(SEQ, D))

    @pl.when(i == pl.num_programs(0) - 1)
    def _():
        lr = lr_ref[0]
        w_ref[:, 0:384] = (wqkv_ref[...].astype(F32) - lr * aq_ref[...].T).astype(BF)
        no = (wo_ref[...].astype(F32) - lr * ao_ref[...]).astype(BF)
        for c in range(D // 128):
            w_ref[c * 128:(c + 1) * 128, 384:512] = no[:, c * 128:(c + 1) * 128]


def dw_attn(lr, n_all, g4, d_all, o_all, wqkv_s, wo_s):
    full = lambda shape: pl.BlockSpec(shape, lambda i: (0, 0))
    gs = g4.shape
    return pl.pallas_call(
        dw_attn_kernel, grid=(NDEV,),
        in_specs=[pl.BlockSpec(memory_space=pltpu.SMEM), pl.BlockSpec((SEQ, D), lambda i: (i, 0)),
                  pl.BlockSpec((gs[0], None, gs[2], D), lambda i: (0, i, 0, 0)),
                  pl.BlockSpec((None, SEQ, 384), lambda i: (i, 0, 0)), pl.BlockSpec((None, SEQ, 128), lambda i: (i, 0, 0)),
                  full((D, 384)), full((128, D))],
        out_specs=full((D, 512)), out_shape=jax.ShapeDtypeStruct((D, 512), BF),
        scratch_shapes=[pltpu.VMEM((384, D), F32), pltpu.VMEM((128, D), F32)],
        cost_estimate=pl.CostEstimate(flops=2 * NDEV * SEQ * D * 512, bytes_accessed=24 << 20, transcendentals=0),
        name="dw_attn",
    )(lr, n_all, g4, d_all, o_all, wqkv_s, wo_s)


def place_mlp_kernel(w_ref, *rest):
    u_ref, d_ref = rest[-2:]
    u_ref[...] = w_ref[0:D]
    d_ref[:, :FB] = w_ref[D:D + FB]
    d_ref[:, FB:] = w_ref[D + FB:]


def place_mlp(l, layers, w_all, prev):
    prev = list(prev)
    ff = NDEV * FB
    return pl.pallas_call(
        place_mlp_kernel, grid=(NDEV,),
        in_specs=[pl.BlockSpec((2 * D, FB), lambda i: (i, 0))] + [ANY] * len(prev),
        out_specs=[pl.BlockSpec((None, D, FB), lambda i: (l, 0, i)), pl.BlockSpec((None, FB, D), lambda i: (l, i, 0))],
        out_shape=[jax.ShapeDtypeStruct((layers, D, ff), BF), jax.ShapeDtypeStruct((layers, ff, D), BF)],
        input_output_aliases={1 + i: i for i in range(len(prev))},
        cost_estimate=pl.CostEstimate(flops=1 << 30, bytes_accessed=32 << 20, transcendentals=0),
        name="place_mlp",
    )(w_all, *prev)


def place_attn_kernel(w_ref, *rest):
    q_ref, k_ref, v_ref, o_ref = rest[-4:]
    q_ref[...] = w_ref[:, 0:128]
    k_ref[...] = w_ref[:, 128:256]
    v_ref[...] = w_ref[:, 256:384]
    for c in range(D // 128):
        o_ref[:, c * 128:(c + 1) * 128] = w_ref[c * 128:(c + 1) * 128, 384:512]


def place_attn(l, layers, w_all, prev):
    prev = list(prev)
    col = pl.BlockSpec((None, D, 128), lambda i: (l, 0, i))
    return pl.pallas_call(
        place_attn_kernel, grid=(NDEV,),
        in_specs=[pl.BlockSpec((D, 512), lambda i: (i, 0))] + [ANY] * len(prev),
        out_specs=[col, col, col, pl.BlockSpec((None, 128, D), lambda i: (l, i, 0))],
        out_shape=[jax.ShapeDtypeStruct((layers, D, D), BF)] * 4,
        input_output_aliases={1 + i: i for i in range(len(prev))},
        cost_estimate=pl.CostEstimate(flops=1 << 30, bytes_accessed=16 << 20, transcendentals=0),
        name="place_attn",
    )(w_all, *prev)


def solution(mesh):
    act_spec = P("dp", "sp", None)
    out_four = P("dp", None, None, None)
    out_three = P("dp", None, None)

    def step(hidden_in, positions, grad_y, w_query, w_key, w_value, w_out, w_up, w_down, gain, learn_rate):
        layers = w_query.shape[0]
        idx = lax.axis_index("sp")
        chunk = SEQ // NDEV
        lr = learn_rate.reshape(1)

        def gather(t):
            return lax.all_gather(t, "sp", axis=0, tiled=True)

        gy_all = lax.all_gather(grad_y, "sp", axis=0, tiled=False)
        pos_tile = jnp.zeros((8, 128), jnp.int32).at[0, :chunk].set(positions)
        x_in, pos_all = entry(hidden_in, jnp.broadcast_to(pos_tile, (NDEV, 8, 128)))
        pos = pos_all[:, 0, :chunk].reshape(SEQ)
        lane = jnp.arange(128, dtype=jnp.int32)
        freqs = ROPE_BASE ** (-(lane % (HD // 2)).astype(F32) / (HD // 2))
        angles = pos.astype(F32)[:, None] * freqs[None, :]
        c_tab = jnp.cos(angles)
        s_tab = jnp.sin(angles) * jnp.where(lane % HD < HD // 2, -1.0, 1.0)[None, :]

        wq = w_query.reshape(layers, D, D)
        wk = w_key.reshape(layers, D, D)
        wv = w_value.reshape(layers, D, D)
        wo = w_out.reshape(layers, D, D)

        saved = []
        hidden = x_in.reshape(SEQ, D)
        normed = norm_apply(hidden.astype(F32), gain[0]).astype(BF)
        for l in range(layers):
            last = l == layers - 1
            q, k, v, o, o_pack, lse = attn_fwd(l, normed, wq, wk, wv, c_tab, s_tab)
            gain_next = gain[min(l + 1, layers - 1)].reshape(1, D)
            out = mlp_fwd(l, last, normed, hidden, o, wo, w_up, w_down, gain_next, o_pack)
            saved.append((hidden, gather(normed), q, k, v, lse, out[2], out[0]))
            hidden = out[1]
            if not last:
                normed = out[3]
        seq_out = hidden.reshape(NDEV, chunk, D)

        grad_h = lax.dynamic_index_in_dim(gy_all, idx, 1, keepdims=False).reshape(SEQ, D)
        g4 = gy_all
        mlp_new, attn_new, seq_res = (), (), []
        for l in reversed(range(layers)):
            hidden_prev, n_all, q, k, v, lse, o_all, pre = saved[l]
            dn_attn, d_pack = attn_bwd(l, grad_h, wo, wq, wk, wv, q, k, v, lse, c_tab, s_tab)
            grad_h = mlp_bwd(l, grad_h, pre, w_up, w_down, dn_attn, hidden_prev, gain[l].reshape(1, D))
            if l > 0:
                g_next = gather(grad_h).reshape(1, NDEV, SEQ, D)
            else:
                seq_out = grad_h.reshape(NDEV, chunk, D)
            wu_s = lax.dynamic_slice(w_up, (l, 0, idx * FB), (1, D, FB))[0]
            wd_s = lax.dynamic_slice(w_down, (l, idx * FB, 0), (1, FB, D))[0]
            wqkv_s = jnp.concatenate([lax.dynamic_slice(w, (l, 0, idx * 128), (1, D, 128))[0] for w in (wq, wk, wv)], axis=1)
            wo_s = lax.dynamic_slice(wo, (l, idx * 128, 0), (1, 128, D))[0]
            w_mlp, d_all, seq_in = dw_mlp(l, lr, n_all, g4, wu_s, wd_s, d_pack, seq_out)
            seq_res.append(seq_in)
            w_attn = dw_attn(lr, n_all, g4, d_all, o_all, wqkv_s, wo_s)
            mlp_new = place_mlp(l, layers, gather(w_mlp), mlp_new)
            attn_new = place_attn(l, layers, gather(w_attn), attn_new)
            if l > 0:
                g4 = g_next
        out_y, grad_x = seq_res[0], seq_res[-1]
        nq, nk, nv, no = attn_new
        return (out_y, grad_x, nq.reshape(w_query.shape), nk.reshape(w_query.shape), nv.reshape(w_query.shape),
                no.reshape(w_out.shape), mlp_new[0], mlp_new[1])

    return jax.shard_map(step, mesh=mesh,
                         in_specs=(act_spec, P(("dp", "sp")), act_spec, P(), P(), P(), P(), P(), P(), P(), P()),
                         out_specs=(act_spec, act_spec, out_four, out_four, out_four, out_four, out_three, out_three),
                         check_vma=False)
```

time: 1890 us -> 654 us (0.35)
  waiting for transfers between devices: 1080 us -> 171 us
  Pallas kernels: 0 us -> 396 us
  matrix products: 326 us -> 0 us
  local copies, waits for them, and re-layouts: 263 us -> 54.7 us
  other arithmetic: 132 us -> 7.4 us
  starting transfers between devices: 58.5 us -> 0.49 us
    psum x1 -> x0, waiting for transfers between devices: 1070 us -> none  [apply_update(): total_grad = lax.psum(local_grad, 'sp')]
    pallas_call x0 -> x17, Pallas kernels: none -> 396 us  [the longest x2 122 us: dw_mlp(): pl.pallas_call(dw_mlp_kernel, grid=(NDEV,), in_specs=[pl.BlockSpec(memory...]
    dot_general x48 -> x0, matrix products: 326 us -> none  [the longest x2 30.5 us: step(): jnp.einsum('bsf,bsd->fd', act_out, grad_h, preferred_element_type=jnp.flo...]
    all_gather x0 -> x8, waiting for transfers between devices: none -> 168 us  [the longest x7 168 us: gather(): return lax.all_gather(t, 'sp', axis=0, tiled=True)]
    unnamed x200 -> x12, local copies, waits for them, and re-layouts: 132 us -> 1.96 us
    another operation x18 -> x0, other arithmetic: 107 us -> none
    convert_element_type x14 -> x1, local copies, waits for them, and re-layouts: 58.8 us -> 0.08 us  [step(): angles = pos.astype(F32)[:, None] * freqs[None, :]]
    all_to_all x16 -> x0, starting transfers between devices: 58.5 us -> none  [the longest x8 29.4 us: to_heads(): return lax.all_to_all(tensor, 'sp', 2, 1, tiled=True)]
  transfers between devices with their start and end apart: 17 -> 8, of which waited for: 3 -> 3; matrix products, arithmetic and copies ran while one was open for 23% -> 9% of each run, Pallas kernels for 0% -> 59%
where the time goes in v1:
time: 654 us; the launch traced here: 645 us
  Pallas kernels  396 us (61%)
  waiting for transfers between devices  171 us (26%)
  local copies, waits for them, and re-layouts  54.7 us (8%)
  between operations  15.4 us (2%)
  other arithmetic  7.4 us (1%)
    all_gather x7, waiting for transfers between devices, gather(): return lax.all_gather(t, 'sp', axis=0, tiled=True)  168 us
    pallas_call x2, Pallas kernels, dw_mlp(): pl.pallas_call(dw_mlp_kernel, grid=(NDEV,), in_specs=[pl.BlockSpec(memory...  122 us
    pallas_call x2, Pallas kernels, mlp_fwd(): pl.pallas_call(functools.partial(mlp_fwd_kernel, last), grid=(ff // FB,),...  53.1 us
    pallas_call x2, Pallas kernels, attn_bwd(): pl.pallas_call(attn_bwd_kernel, grid=(nb,), in_specs=[full((SEQ, D)), pl....  51.3 us
    pallas_call x2, Pallas kernels, mlp_bwd(): pl.pallas_call(mlp_bwd_kernel, grid=(ff // FB,), in_specs=[full((SEQ, D))...  39.4 us
    pallas_call x2, Pallas kernels, attn_fwd(): pl.pallas_call(attn_fwd_kernel, grid=(nb,), in_specs=[full((SEQ, D)), wsp...  33.2 us
    pallas_call x2, Pallas kernels, place_mlp(): pl.pallas_call(place_mlp_kernel, grid=(NDEV,), in_specs=[pl.BlockSpec((2...  27.8 us
    pallas_call x2, Pallas kernels, dw_attn(): pl.pallas_call(dw_attn_kernel, grid=(NDEV,), in_specs=[pl.BlockSpec(memor...  26.2 us
  transfers between devices with their start and end apart: 8, of which 3 were waited for; matrix products, arithmetic and copies ran while one was open for 9% of the time, Pallas kernels for 59%

profile of v1, /device:TPU:1, one launch (start us, length us, event | category | flops | bytes accessed | tf_op | source)
XLA Modules:
  0.0 645.1 jit_solution(12781089128673158721)
XLA Ops:
  9.2 24.0 %entry.1 = (bf16[8,64,1024]{2,1,0:T(8,128)(2,1)}, s32[8,8,128]{2,1,0:T(8,128)}) custom-call(bf16[8,64,1024]{2,1,0:T(8,128)(2,1)} %x_ref.1, s32[8,8,128]{2,1,0:T(8,128)} %broadcast_in_dim.16.p_ref), custom_call_target="tpu_custom_call" | custom-call | tf_op jit(solution)/shard_map/entry/pallas_call | solution.py:234
  34.1 1.5 multiply_reduce_fusion
  35.7 6.2 copy.52.wq_ref
  41.9 6.2 copy.53.wk_ref
  48.0 6.3 copy.54.wv_ref
  54.9 1.8 fusion
  58.0 16.6 %attn_fwd.2 = (bf16[512,1024]{1,0:T(8,128)(2,1)}, bf16[512,1024]{1,0:T(8,128)(2,1)}, bf16[512,1024]{1,0:T(8,128)(2,1)}, bf16[512,1024]{1,0:T(8,128)(2,1)}, bf16[...) custom-call(bf16[512,1024]{1,0:T(8,128)(2,1)} %multiply_convert_fusion.n_ref, bf16[2,1024,1024]{2,1,0:T(8,128)(2,1)} %copy.52.wq_ref, ...), custom_call_target="tpu_custom_call" | custom-call | flops 5368709120 | bytes 14680064 | tf_op jit(solution)/shard_map/attn_fwd/pallas_call | solution.py:92
  74.6 22.5 %mlp_fwd.2 = (f32[512,4096]{1,0:T(8,128)}, bf16[512,1024]{1,0:T(8,128)(2,1)}, bf16[8,512,128]{2,1,0:T(8,128)(2,1)}, bf16[512,1024]{1,0:T(8,128)(2,1)}) custom-call(bf16[512,1024]{1,0:T(8,128)(2,1)} %multiply_convert_fusion.n_ref, bf16[512,1024]{1,0:T(8,128)(2,1)} %bitcast.45, bf16[512,1024]{1,0:T(8,128)(2,1)} %get-tuple-element.65.o_ref, ...), custom_call_target="tpu_custom_call" | custom-call | flops 9663676416 | bytes 31457280 | tf_op jit(solution)/shard_map/mlp_fwd/pallas_call | solution.py:294
  98.2 16.6 %attn_fwd.3 = (bf16[512,1024]{1,0:T(8,128)(2,1)}, bf16[512,1024]{1,0:T(8,128)(2,1)}, bf16[512,1024]{1,0:T(8,128)(2,1)}, bf16[512,1024]{1,0:T(8,128)(2,1)}, bf16[...) custom-call(bf16[512,1024]{1,0:T(8,128)(2,1)} %get-tuple-element.67.n_ref, bf16[2,1024,1024]{2,1,0:T(8,128)(2,1)} %copy.52.wq_ref, ...), custom_call_target="tpu_custom_call" | custom-call | flops 5368709120 | bytes 14680064 | tf_op jit(solution)/shard_map/attn_fwd/pallas_call | solution.py:92
  114.8 30.6 %mlp_fwd.3 = (f32[512,4096]{1,0:T(8,128)}, bf16[512,1024]{1,0:T(8,128)(2,1)}, bf16[8,512,128]{2,1,0:T(8,128)(2,1)}) custom-call(bf16[512,1024]{1,0:T(8,128)(2,1)} %get-tuple-element.67.n_ref, bf16[512,1024]{1,0:T(8,128)(2,1)} %get-tuple-element.73.x_ref, bf16[512,1024]{1,0:T(8,128)(2,1)} %get-tuple-element.74.o_ref, bf16[2,1024,1024]{2,1,0:T(8,128)(2,1)} %bitcast.41, ...), custom_call_target="tpu_custom_call" | custom-call | flops 9663676416 | bytes 31457280 | tf_op jit(solution)/shard_map/mlp_fwd/pallas_call | solution.py:294
  145.4 2.3 constant_dynamic-slice_fusion.6
  147.7 25.5 %attn_bwd.2 = (f32[512,1024]{1,0:T(8,128)}, bf16[8,512,384]{2,1,0:T(8,128)(2,1)}) custom-call(bf16[512,1024]{1,0:T(8,128)(2,1)} %bitcast.58, bf16[2,1024,1024]{2,1,0:T(8,128)(2,1)} %bitcast.42, bf16[2,1024,1024]{2,1,0:T(8,128)(2,1)} %copy.52.wq_ref, bf16[2,1024,1024]{2,1,0:T(8,128)(2,1)} %copy.53.wk_ref, bf16[2,1024,1024]{2,1,0:T(8,128)(2,1)} %copy.54.wv_ref, ...), custom_call_target="tpu_custom_call" | custom-call | flops 9663676416 | bytes 20971520 | tf_op jit(solution)/shard_map/attn_bwd/pallas_call | solution.py:176
  173.2 19.8 %mlp_bwd.2.g_ref = bf16[512,1024]{1,0:T(8,128)(2,1)} custom-call(bf16[512,1024]{1,0:T(8,128)(2,1)} %bitcast.59, f32[512,4096]{1,0:T(8,128)} %get-tuple-element.78.pre_ref, bf16[2,1024,4096]{2,1,0:T(8,128)(2,1)} %wu_ref.7, bf16[2,4096,1024]{2,1,0:T(8,128)(2,1)} %wd_ref.7, f32[512,1024]{1,0:T(8,128)} %get-tuple-element.79.dn_ref, ...), custom_call_target="tpu_custom_call" | custom-call | flops 8589934592 | bytes 31457280 | tf_op jit(solution)/shard_map/mlp_bwd/pallas_call | solution.py:331
  196.6 1.9 dynamic-slice_bitcast_fusion.4
  199.6 3.0 dynamic-slice_bitcast_fusion.1
  202.6 3.0 dynamic-slice_bitcast_fusion
  205.6 70.7 %dw_mlp.2 = (bf16[2048,512]{1,0:T(8,128)(2,1)}, bf16[8,512,384]{2,1,0:T(8,128)(2,1)}, bf16[8,64,1024]{2,1,0:T(8,128)(2,1)}) custom-call(f32[1]{0:T(128)} %bitcast.36.lr_ref, bf16[4096,1024]{1,0:T(8,128)(2,1)} %all-gather.10.cloned.1.call-done.n_ref, bf16[8,8,64,1024]{3,2,1,0:T(8,128)(2,1)} %bitcast.48, bf16[1024,512]{1,0:T(8,128)(2,1)} %get-tuple-element.117.wu_ref, ...), custom_call_target="tpu_custom_call" | custom-call | flops 17179869184 | bytes 25165824 | tf_op jit(solution)/shard_map/dw_mlp/pallas_call | solution.py:378
  276.3 13.0 %dw_attn.3 = bf16[1024,512]{1,0:T(8,128)(2,1)} custom-call(f32[1]{0:T(128)} %bitcast.39.lr_ref, bf16[4096,1024]{1,0:T(8,128)(2,1)} %all-gather.10.cloned.1.call-done.n_ref, bf16[8,8,64,1024]{3,2,1,0:T(8,128)(2,1)} %bitcast.49, bf16[8,512,384]{2,1,0:T(8,128)(2,1)} %get-tuple-element.90.d_ref, bf16[8,512,128]{2,1,0:T(8,128)(2,1)} %get-tuple-element.91.o_ref, ...), custom_call_target="tpu_custom_call" | custom-call | flops 4294967296 | bytes 25165824 | tf_op jit(solution)/shard_map/dw_attn/pallas_call | solution.py:415
  290.9 25.8 %attn_bwd.3 = (f32[512,1024]{1,0:T(8,128)}, bf16[8,512,384]{2,1,0:T(8,128)(2,1)}) custom-call(bf16[512,1024]{1,0:T(8,128)(2,1)} %mlp_bwd.2.g_ref, bf16[2,1024,1024]{2,1,0:T(8,128)(2,1)} %bitcast.44, bf16[2,1024,1024]{2,1,0:T(8,128)(2,1)} %copy.52.wq_ref, bf16[2,1024,1024]{2,1,0:T(8,128)(2,1)} %copy.53.wk_ref, bf16[2,1024,1024]{2,1,0:T(8,128)(2,1)} %copy.54.wv_ref, ...), custom_call_target="tpu_custom_call" | custom-call | flops 9663676416 | bytes 20971520 | tf_op jit(solution)/shard_map/attn_bwd/pallas_call | solution.py:176
  316.7 19.6 %mlp_bwd.3 = bf16[512,1024]{1,0:T(8,128)(2,1)} custom-call(bf16[512,1024]{1,0:T(8,128)(2,1)} %mlp_bwd.2.g_ref, f32[512,4096]{1,0:T(8,128)} %get-tuple-element.85.pre_ref, bf16[2,1024,4096]{2,1,0:T(8,128)(2,1)} %wu_ref.7, bf16[2,4096,1024]{2,1,0:T(8,128)(2,1)} %wd_ref.7, f32[512,1024]{1,0:T(8,128)} %get-tuple-element.86.dn_ref, bf16[512,1024]{1,0:T(8,128)(2,1)} %bitcast.46, ...), custom_call_target="tpu_custom_call" | custom-call | flops 8589934592 | bytes 31457280 | tf_op jit(solution)/shard_map/mlp_bwd/pallas_call | solution.py:331
  336.3 51.3 %dw_mlp.3 = (bf16[2048,512]{1,0:T(8,128)(2,1)}, bf16[8,512,384]{2,1,0:T(8,128)(2,1)}, bf16[8,64,1024]{2,1,0:T(8,128)(2,1)}) custom-call(f32[1]{0:T(128)} %bitcast.37.lr_ref, bf16[4096,1024]{1,0:T(8,128)(2,1)} %all-gather.12.cloned.1.call-done.n_ref, bf16[1,8,512,1024]{3,2,1,0:T(8,128)(2,1)} %bitcast.50, bf16[1024,512]{1,0:T(8,128)(2,1)} %get-tuple-element.116.wu_ref, ...), custom_call_target="tpu_custom_call" | custom-call | flops 17179869184 | bytes 25165824 | tf_op jit(solution)/shard_map/dw_mlp/pallas_call | solution.py:378
  387.6 13.2 %dw_attn.2 = bf16[1024,512]{1,0:T(8,128)(2,1)} custom-call(f32[1]{0:T(128)} %bitcast.38.lr_ref, bf16[4096,1024]{1,0:T(8,128)(2,1)} %all-gather.12.cloned.1.call-done.n_ref, bf16[1,8,512,1024]{3,2,1,0:T(8,128)(2,1)} %bitcast.51, bf16[8,512,384]{2,1,0:T(8,128)(2,1)} %get-tuple-element.88.d_ref, bf16[8,512,128]{2,1,0:T(8,128)(2,1)} %get-tuple-element.89.o_ref, ...), custom_call_target="tpu_custom_call" | custom-call | flops 4294967296 | bytes 25165824 | tf_op jit(solution)/shard_map/dw_attn/pallas_call | solution.py:415
  402.4 9.4 %place_attn.2 = (bf16[2,1024,1024]{2,1,0:T(8,128)(2,1)}, bf16[2,1024,1024]{2,1,0:T(8,128)(2,1)}, bf16[2,1024,1024]{2,1,0:T(8,128)(2,1)}, bf16[2,1024,1024]{2,1,0:T(8,128)(2,1)}) custom-call(bf16[8192,512]{1,0:T(8,128)(2,1)} %all-gather.18.cloned.1.call-done.w_ref), custom_call_target="tpu_custom_call" | custom-call | flops 1073741824 | bytes 16777216 | tf_op jit(solution)/shard_map/place_attn/pallas_call | solution.py:461
  411.8 38.2 %all-gather.16.cloned.1.call-done.w_ref = bf16[8192,512]{1,0:T(8,128)(2,1)} async-done(((bf16[1024,512]{1,0:T(8,128)(2,1)}), bf16[8192,512]{1,0:T(8,128)(2,1)}) %all-gather.16.cloned.1.call-update) | async-done | bytes 8388624 | tf_op jit(solution)/shard_map/all_gather | solution.py:484
  450.1 9.4 %place_attn.3 = (bf16[2,1024,1024]{2,1,0:T(8,128)(2,1)}, bf16[2,1024,1024]{2,1,0:T(8,128)(2,1)}, bf16[2,1024,1024]{2,1,0:T(8,128)(2,1)}, bf16[2,1024,1024]{2,1,0:T(8,128)(2,1)}) custom-call(bf16[8192,512]{1,0:T(8,128)(2,1)} %all-gather.16.cloned.1.call-done.w_ref, ...), custom_call_target="tpu_custom_call", output_to_operand_aliasing={{0}: (1, {}), {1}: (2, {}), {2}: (3, {}), {3}: (4, {})} | custom-call | flops 1073741824 | bytes 16777216 | tf_op jit(solution)/shard_map/place_attn/pallas_call | solution.py:461
  459.5 6.2 copy.70
  465.6 6.2 copy.71
  471.8 6.2 copy.72
  478.0 58.0 %all-gather.22.cloned.1.call-done.w_ref = bf16[16384,512]{1,0:T(8,128)(2,1)} async-done(((bf16[2048,512]{1,0:T(8,128)(2,1)}), bf16[16384,512]{1,0:T(8,128)(2,1)}) %all-gather.22.cloned.1.call-update) | async-done | bytes 16777232 | tf_op jit(solution)/shard_map/all_gather | solution.py:484
  536.0 13.8 %place_mlp.2 = (bf16[2,1024,4096]{2,1,0:T(8,128)(2,1)}, bf16[2,4096,1024]{2,1,0:T(8,128)(2,1)}) custom-call(bf16[16384,512]{1,0:T(8,128)(2,1)} %all-gather.22.cloned.1.call-done.w_ref), custom_call_target="tpu_custom_call" | custom-call | flops 1073741824 | bytes 33554432 | tf_op jit(solution)/shard_map/place_mlp/pallas_call | solution.py:438
  549.8 72.1 %all-gather.20.cloned.1.call-done.w_ref = bf16[16384,512]{1,0:T(8,128)(2,1)} async-done(((bf16[2048,512]{1,0:T(8,128)(2,1)}), bf16[16384,512]{1,0:T(8,128)(2,1)}) %all-gather.20.cloned.1.call-update) | async-done | bytes 16777232 | tf_op jit(solution)/shard_map/all_gather | solution.py:484
  621.9 14.0 %place_mlp.3 = (bf16[2,1024,4096]{2,1,0:T(8,128)(2,1)}, bf16[2,4096,1024]{2,1,0:T(8,128)(2,1)}) custom-call(bf16[16384,512]{1,0:T(8,128)(2,1)} %all-gather.20.cloned.1.call-done.w_ref, bf16[2,1024,4096]{2,1,0:T(8,128)(2,1)} %get-tuple-element.102.rest_0_, bf16[2,4096,1024]{2,1,0:T(8,128)(2,1)} %get-tuple-element.103.rest_1_), custom_call_target="tpu_custom_call", output_to_operand_aliasing={{0}: (1, {}), {1}: (2, {})} | custom-call | flops 1073741824 | bytes 33554432 | tf_op jit(solution)/shard_map/place_mlp/pallas_call | solution.py:438
  (52 shorter events, 14.8 us)
Async XLA Ops:
  7.2 138.2 %all-gather.24.cloned.1.call-start = ((), (), s32[]{:S(2)}) async-start(), calls=%async_computation.7 | async-start | bytes 9437184 | tf_op jit(solution)/shard_map/all_gather | solution.py:486
  7.9 197.7 %all-gather.10.cloned.1.call-start = ((), (), s32[]{:S(2)}) async-start(), calls=%async_computation | async-start | bytes 9437184 | tf_op jit(solution)/shard_map/all_gather | solution.py:484
  48.0 6.3 copy-start.4
  48.0 8.7 %copy-start = (bf16[8,64,1024]{2,1,0:T(8,128)(2,1)S(1)}, bf16[8,64,1024]{2,1,0:T(8,128)(2,1)}, u32[]{:S(2)}) copy-start(bf16[8,64,1024]{2,1,0:T(8,128)(2,1)} %get-tuple-element.63) | copy-start | bytes 3145732
  54.9 19.7 %copy-start.3 = (f32[1,1024]{1,0:T(1,128)}, f32[1,1024]{1,0:T(1,128)S(1)}, u32[]{:S(2)}) copy-start(f32[1,1024]{1,0:T(1,128)S(1)} %get-tuple-element.127.gain_ref) | copy-start | bytes 12292
  97.2 239.1 %all-gather.12.cloned.1.call-start = ((), (), s32[]{:S(2)}) async-start(), calls=%async_computation.1 | async-start | bytes 9437184 | tf_op jit(solution)/shard_map/all_gather | solution.py:484
  97.9 238.4 %all-gather.14.cloned.1.call-start = ((), (), s32[]{:S(2)}) async-start(), calls=%async_computation.2 | async-start | bytes 9437184 | tf_op jit(solution)/shard_map/all_gather | solution.py:484
  193.1 209.3 %all-gather.18.cloned.1.call-start = ((), (), s32[]{:S(2)}) async-start(), calls=%async_computation.4 | async-start | bytes 9437184 | tf_op jit(solution)/shard_map/all_gather | solution.py:484
  289.3 160.7 %all-gather.16.cloned.1.call-start = ((), (), s32[]{:S(2)}) async-start(), calls=%async_computation.3 | async-start | bytes 9437184 | tf_op jit(solution)/shard_map/all_gather | solution.py:484
  400.9 135.1 %all-gather.22.cloned.1.call-start = ((), (), s32[]{:S(2)}) async-start(), calls=%async_computation.6 | async-start | bytes 18874368 | tf_op jit(solution)/shard_map/all_gather | solution.py:484
  401.6 220.3 %all-gather.20.cloned.1.call-start = ((), (), s32[]{:S(2)}) async-start(), calls=%async_computation.5 | async-start | bytes 18874368 | tf_op jit(solution)/shard_map/all_gather | solution.py:484
  621.9 14.0 %copy-start.1 = (bf16[8,64,1024]{2,1,0:T(8,128)(2,1)S(1)}, bf16[8,64,1024]{2,1,0:T(8,128)(2,1)}, u32[]{:S(2)}) copy-start(bf16[8,64,1024]{2,1,0:T(8,128)(2,1)} %get-tuple-element.142) | copy-start | bytes 3145732
  621.9 15.0 %copy-start.2 = (bf16[8,64,1024]{2,1,0:T(8,128)(2,1)S(1)}, bf16[8,64,1024]{2,1,0:T(8,128)(2,1)}, u32[]{:S(2)}) copy-start(bf16[8,64,1024]{2,1,0:T(8,128)(2,1)} %get-tuple-element.143) | copy-start | bytes 3145732
Sparse Core Ops, SparseCore 0:
  9.8 56.5 all-gather.23
  97.3 58.7 all-gather.9
  158.5 48.3 all-gather.11
  208.6 83.0 all-gather.13
  293.4 48.6 all-gather.17
  401.0 49.0 all-gather.15
  451.9 84.0 all-gather.21
  537.8 84.0 all-gather.19

commit v2 on v1

v2 whole, which is shorter than its diff:
```python
import functools
import jax
import jax.numpy as jnp
from jax import lax
from jax.experimental import pallas as pl
from jax.experimental.pallas import tpu as pltpu
from jax.sharding import PartitionSpec as P

EPSILON = 1e-6
ROPE_BASE = 10000.0
NEG_LARGE = -1e30
HD = 64
SEQ = 512
LANE = 128
QKV = 384
D = 1024
CB = 256
QB = 256
BF = jnp.bfloat16
F32 = jnp.float32


ANY = pl.BlockSpec(memory_space=pl.ANY)
SMEM = pl.BlockSpec(memory_space=pltpu.SMEM)


def full(*shape):
    return pl.BlockSpec(shape, lambda i: (0, 0))


def cost(flops, mib):
    return pl.CostEstimate(flops=flops, bytes_accessed=mib << 20, transcendentals=0)


def norm_apply(x_f32, gain_row):
    inv_rms = lax.rsqrt(jnp.mean(x_f32 * x_f32, axis=-1, keepdims=True) + EPSILON)
    return x_f32 * inv_rms * gain_row


def dot_nn(a, b):
    return lax.dot_general(a, b, (((1,), (0,)), ((), ())), preferred_element_type=F32)


def dot_nt(a, b):
    return lax.dot_general(a, b, (((1,), (1,)), ((), ())), preferred_element_type=F32)


def swap_halves(t):
    lane = lax.broadcasted_iota(jnp.int32, t.shape, 1)
    return jnp.where(lane % HD < HD // 2, pltpu.roll(t, t.shape[1] - HD // 2, 1), pltpu.roll(t, HD // 2, 1))


def head_mask(rows, h):
    lane = lax.broadcasted_iota(jnp.int32, (rows, LANE), 1)
    return lane < HD if h % 2 == 0 else lane >= HD


def causal_mask(nk, j):
    key = lax.broadcasted_iota(jnp.int32, (nk, QB), 0)
    qry = lax.broadcasted_iota(jnp.int32, (nk, QB), 1) + j * QB
    return key <= qry


def attn_fwd_kernel(n_ref, wq_ref, wk_ref, wv_ref, c_ref, s_ref, q_ref, k_ref, v_ref, o_ref, op_ref, lse_ref):
    n = n_ref[...]
    c = jnp.concatenate([c_ref[...]] * (CB // LANE), axis=1)
    s = jnp.concatenate([s_ref[...]] * (CB // LANE), axis=1)
    qf = dot_nn(n, wq_ref[...])
    q = (qf * c + swap_halves(qf) * s).astype(BF)
    kf = dot_nn(n, wk_ref[...])
    k = (kf * c + swap_halves(kf) * s).astype(BF)
    v = dot_nn(n, wv_ref[...]).astype(BF)
    q_ref[...] = q
    k_ref[...] = k
    v_ref[...] = v
    vt = v.T
    heads = []
    for h in range(CB // HD):
        lo = (h // 2) * LANE
        qm = jnp.where(head_mask(SEQ, h), q[:, lo:lo + LANE] * BF(HD ** -0.5), BF(0))
        k2 = k[:, lo:lo + LANE]
        cols = []
        for j in range(SEQ // QB):
            nk = (j + 1) * QB
            st = dot_nt(k2[:nk], qm[j * QB:(j + 1) * QB])
            st = jnp.where(causal_mask(nk, j), st, NEG_LARGE)
            m = jnp.max(st, axis=0, keepdims=True)
            e = jnp.exp(st - m)
            l = jnp.sum(e, axis=0, keepdims=True)
            p = (e * (1.0 / l)).astype(BF)
            cols.append(dot_nn(vt[h * HD:(h + 1) * HD, :nk], p))
            lse_ref[h:h + 1, j * QB:(j + 1) * QB] = m + jnp.log(l)
        heads.append(jnp.concatenate(cols, axis=1))
    o = jnp.concatenate(heads, axis=0).T.astype(BF)
    o_ref[...] = o
    op_ref[0] = o[:, :LANE]
    op_ref[1] = o[:, LANE:]


def attn_fwd(l, n, wq, wk, wv, c, s):
    nb = D // CB
    wspec = pl.BlockSpec((None, D, CB), lambda i: (l, 0, i))
    aspec = pl.BlockSpec((SEQ, CB), lambda i: (0, i))
    act = jax.ShapeDtypeStruct((SEQ, D), BF)
    return pl.pallas_call(
        attn_fwd_kernel,
        grid=(nb,),
        in_specs=[full(SEQ, D), wspec, wspec, wspec, full(SEQ, LANE), full(SEQ, LANE)],
        out_specs=[aspec, aspec, aspec, aspec, pl.BlockSpec((2, SEQ, LANE), lambda i: (i, 0, 0)),
                   pl.BlockSpec((None, CB // HD, SEQ), lambda i: (i, 0, 0))],
        out_shape=[act, act, act, act, jax.ShapeDtypeStruct((8, SEQ, LANE), BF),
                   jax.ShapeDtypeStruct((nb, CB // HD, SEQ), F32)],
        cost_estimate=cost(6 * SEQ * D * D + 8 * SEQ * SEQ * D, 14),
        name="attn_fwd",
    )(n, wq, wk, wv, c, s)


def attn_bwd_kernel(g_ref, wo_ref, wq_ref, wk_ref, wv_ref, q_ref, k_ref, v_ref, lse_ref, c_ref, s_ref, dn_ref, dp_ref):
    do = dot_nt(g_ref[...], wo_ref[...]).astype(BF)
    q = q_ref[...]
    k = k_ref[...]
    v = v_ref[...]
    kt = k.T
    dqs, dks, dvs = [], [], []
    for h in range(CB // HD):
        lo = (h // 2) * LANE
        hm = head_mask(SEQ, h)
        q2 = q[:, lo:lo + LANE]
        qm = jnp.where(hm, q2 * BF(HD ** -0.5), BF(0))
        do2 = do[:, lo:lo + LANE]
        dom = jnp.where(hm, do2, BF(0))
        k2 = k[:, lo:lo + LANE]
        v2 = v[:, lo:lo + LANE]
        dk = dv = None
        cols = []
        for j in reversed(range(SEQ // QB)):
            nk = (j + 1) * QB
            rows = slice(j * QB, (j + 1) * QB)
            st = dot_nt(k2[:nk], qm[rows])
            pt = jnp.where(causal_mask(nk, j), jnp.exp(st - lse_ref[h:h + 1, rows]), 0.0)
            dpt = dot_nt(v2[:nk], dom[rows])
            rd = jnp.sum(dpt * pt, axis=0, keepdims=True)
            dst = (pt * (dpt - rd) * HD ** -0.5).astype(BF)
            dv_j = dot_nn(pt.astype(BF), do2[rows])
            dk_j = dot_nn(dst, q2[rows])
            cols.append(dot_nn(kt[h * HD:(h + 1) * HD, :nk], dst))
            if dk is None:
                dk, dv = dk_j, dv_j
            else:
                dk = jnp.concatenate([dk[:nk] + dk_j, dk[nk:]], axis=0)
                dv = jnp.concatenate([dv[:nk] + dv_j, dv[nk:]], axis=0)
        dqs.append(jnp.concatenate(cols[::-1], axis=1))
        dks.append(dk)
        dvs.append(dv)
    c = jnp.concatenate([c_ref[...]] * (CB // LANE), axis=1)
    s = jnp.concatenate([s_ref[...]] * (CB // LANE), axis=1)
    low = head_mask(SEQ, 0)

    def join(parts):
        return jnp.concatenate([jnp.where(low, parts[2 * i], parts[2 * i + 1]) for i in range(CB // LANE)], axis=1).astype(BF)

    def unrope(t):
        t = t.astype(F32)
        return (t * c - swap_halves(t) * s).astype(BF)

    dq = unrope(jnp.concatenate(dqs, axis=0).T.astype(BF))
    dk = unrope(join(dks))
    dv = join(dvs)
    for i in range(2):
        dp_ref[i, :, 0:LANE] = dq[:, i * LANE:(i + 1) * LANE]
        dp_ref[i, :, LANE:256] = dk[:, i * LANE:(i + 1) * LANE]
        dp_ref[i, :, 256:QKV] = dv[:, i * LANE:(i + 1) * LANE]
    dn = dot_nt(dq, wq_ref[...]) + dot_nt(dk, wk_ref[...]) + dot_nt(dv, wv_ref[...])

    @pl.when(pl.program_id(0) == 0)
    def _():
        dn_ref[...] = dn

    @pl.when(pl.program_id(0) > 0)
    def _():
        dn_ref[...] += dn


def attn_bwd(l, g, wo, wq, wk, wv, q, k, v, lse, c, s):
    nb = D // CB
    wspec = pl.BlockSpec((None, D, CB), lambda i: (l, 0, i))
    aspec = pl.BlockSpec((SEQ, CB), lambda i: (0, i))
    return pl.pallas_call(
        attn_bwd_kernel,
        grid=(nb,),
        in_specs=[full(SEQ, D), pl.BlockSpec((None, CB, D), lambda i: (l, i, 0)), wspec, wspec, wspec, aspec, aspec, aspec,
                  pl.BlockSpec((None, CB // HD, SEQ), lambda i: (i, 0, 0)), full(SEQ, LANE), full(SEQ, LANE)],
        out_specs=[full(SEQ, D), pl.BlockSpec((2, SEQ, QKV), lambda i: (i, 0, 0))],
        out_shape=[jax.ShapeDtypeStruct((SEQ, D), F32), jax.ShapeDtypeStruct((8, SEQ, QKV), BF)],
        cost_estimate=cost(8 * SEQ * D * D + 20 * SEQ * SEQ * D, 20),
        name="attn_bwd",
    )(g, wo, wq, wk, wv, q, k, v, lse, c, s)


NDEV = 8
MB = 1024
MESH_ID = pl.DeviceIdType.MESH
FB = 512


def token_spec(t, tile=lambda i: i):
    return pl.BlockSpec((t.shape[0], None, t.shape[2], D), lambda i: (0, tile(i), 0, 0))


class Exchange:
    def __init__(self, pairs, send_sem, recv_sem, local_sem):
        me = lax.axis_index("sp")
        self.remote, self.local = [], []
        for a, (src, dst) in enumerate(pairs):
            self.local.append(pltpu.make_async_copy(src.at[me], dst.at[me], local_sem.at[a]))
        for k in range(1, NDEV):
            peer = lax.rem(me + k, NDEV)
            for a, (src, dst) in enumerate(pairs):
                self.remote.append(pltpu.make_async_remote_copy(
                    src_ref=src.at[peer], dst_ref=dst.at[me], send_sem=send_sem.at[a, k], recv_sem=recv_sem.at[a, k],
                    device_id={"sp": peer}, device_id_type=MESH_ID))

    def start(self):
        me = lax.axis_index("sp")
        barrier = pltpu.get_barrier_semaphore()
        for k in range(1, NDEV):
            pl.semaphore_signal(barrier, inc=1, device_id={"sp": lax.rem(me + k, NDEV)}, device_id_type=MESH_ID)
        for c in self.local:
            c.start()
        pl.semaphore_wait(barrier, NDEV - 1)
        for c in self.remote:
            c.start()

    def wait(self):
        for c in self.local + self.remote:
            c.wait()


def exchange_sems(n):
    return [pltpu.SemaphoreType.DMA((n, NDEV)), pltpu.SemaphoreType.DMA((n, NDEV)), pltpu.SemaphoreType.DMA((n,))]


def share_kernel(p_ref, po_ref, ss, rs, ls):
    ex = Exchange([(p_ref, po_ref)], ss, rs, ls)
    ex.start()
    ex.wait()


def share(pos):
    return pl.pallas_call(
        share_kernel, in_specs=[ANY], out_specs=ANY, out_shape=jax.ShapeDtypeStruct(pos.shape, pos.dtype),
        scratch_shapes=exchange_sems(1),
        compiler_params=pltpu.CompilerParams(collective_id=1, has_side_effects=True), name="share",
    )(pos)


def gelu_parts(x):
    c = 0.7978845608028654
    x2 = x * x
    t = jnp.tanh(c * (x + 0.044715 * (x2 * x)))
    return x2, t, c


def gelu(x):
    _, t, _ = gelu_parts(x)
    return x * (0.5 * (1.0 + t))


def gelu_slope(x):
    x2, t, c = gelu_parts(x)
    return 0.5 * (1.0 + t) + 0.5 * x * (1.0 - t * t) * (c * (1.0 + 3 * 0.044715 * x2))


def mlp_fwd_kernel(last, n_ref, x_ref, o_ref, wo_ref, wu_ref, wd_ref, gain_ref, *rest):
    if last:
        pre_ref, h_ref, acc_ref = rest
    else:
        pre_ref, h_ref, nn_ref, acc_ref = rest
    i = pl.program_id(0)

    @pl.when(i == 0)
    def _():
        acc_ref[...] = x_ref[...].astype(F32) + dot_nn(o_ref[...], wo_ref[...])

    pre = dot_nn(n_ref[...], wu_ref[...])
    pre_ref[...] = pre
    acc_ref[...] += dot_nn(gelu(pre).astype(BF), wd_ref[...])

    @pl.when(i == pl.num_programs(0) - 1)
    def _():
        h = acc_ref[...].astype(BF)
        h_ref[...] = h
        if not last:
            nn_ref[...] = norm_apply(h.astype(F32), gain_ref[...]).astype(BF)


def mlp_fwd(l, last, n, x, o, wo, wu, wd, gain_next):
    ff = wu.shape[2]
    act = jax.ShapeDtypeStruct((SEQ, D), BF)
    out_specs = [pl.BlockSpec((SEQ, MB), lambda i: (0, i)), full(SEQ, D)]
    out_shape = [jax.ShapeDtypeStruct((SEQ, ff), F32), act]
    if not last:
        out_specs.append(full(SEQ, D))
        out_shape.append(act)
    return pl.pallas_call(
        functools.partial(mlp_fwd_kernel, last), grid=(ff // MB,),
        in_specs=[full(SEQ, D), full(SEQ, D), full(SEQ, D), pl.BlockSpec((None, D, D), lambda i: (l, 0, 0)),
                  pl.BlockSpec((None, D, MB), lambda i: (l, 0, i)), pl.BlockSpec((None, MB, D), lambda i: (l, i, 0)),
                  full(1, D)],
        out_specs=out_specs, out_shape=out_shape,
        scratch_shapes=[pltpu.VMEM((SEQ, D), F32)],
        cost_estimate=cost(4 * SEQ * D * ff + 2 * SEQ * D * D, 30),
        name="mlp_fwd",
    )(n, x, o, wo, wu, wd, gain_next)


def mlp_bwd_kernel(g_ref, pre_ref, wu_ref, wd_ref, dn_ref, x_ref, gain_ref, go_ref, acc_ref):
    i = pl.program_id(0)

    @pl.when(i == 0)
    def _():
        acc_ref[...] = dn_ref[...]

    d_act = dot_nt(g_ref[...], wd_ref[...]).astype(BF)
    d_pre = (d_act.astype(F32) * gelu_slope(pre_ref[...])).astype(BF)
    acc_ref[...] += dot_nt(d_pre, wu_ref[...])

    @pl.when(i == pl.num_programs(0) - 1)
    def _():
        x = x_ref[...].astype(F32)
        r = lax.rsqrt(jnp.mean(x * x, axis=-1, keepdims=True) + EPSILON)
        t = acc_ref[...] * gain_ref[...]
        dot = jnp.mean(x * t, axis=-1, keepdims=True)
        dx = r * t - x * (r * r * r * dot)
        go_ref[...] = (g_ref[...].astype(F32) + dx).astype(BF)


def mlp_bwd(l, g, pre, wu, wd, dn, x, gain_row):
    ff = wu.shape[2]
    return pl.pallas_call(
        mlp_bwd_kernel, grid=(ff // MB,),
        in_specs=[full(SEQ, D), pl.BlockSpec((SEQ, MB), lambda i: (0, i)), pl.BlockSpec((None, D, MB), lambda i: (l, 0, i)),
                  pl.BlockSpec((None, MB, D), lambda i: (l, i, 0)), full(SEQ, D), full(SEQ, D), full(1, D)],
        out_specs=full(SEQ, D), out_shape=jax.ShapeDtypeStruct((SEQ, D), BF),
        scratch_shapes=[pltpu.VMEM((SEQ, D), F32)],
        cost_estimate=cost(4 * SEQ * D * ff, 30),
        name="mlp_bwd",
    )(g, pre, wu, wd, dn, x, gain_row)


def dw_tile(wut, wd, n, g, au_ref, ad_ref):
    pre = dot_nt(wut, n)
    d_act = dot_nt(wd, g).astype(BF)
    x2, t, c = gelu_parts(pre)
    half = 0.5 * (1.0 + t)
    act = (pre * half).astype(BF)
    slope = half + 0.5 * pre * (1.0 - t * t) * (c * (1.0 + 3 * 0.044715 * x2))
    d_pre = (d_act.astype(F32) * slope).astype(BF)
    ad_ref[...] += dot_nn(act, g)
    au_ref[...] += dot_nn(d_pre, n)


def dw_finish(lr, wut, wd, au, ad):
    nu = (wut.astype(F32) - lr * au).astype(BF).T
    nd = (wd.astype(F32) - lr * ad).astype(BF)
    return nu, nd


def load_block(l, col, wu_ref, wd_ref, wu_buf, wd_buf, sem):
    at = pl.ds(pl.multiple_of(col * FB, FB), FB)
    return (pltpu.make_async_copy(wu_ref.at[l, :, at], wu_buf, sem.at[0]),
            pltpu.make_async_copy(wd_ref.at[l, at, :], wd_buf, sem.at[1]))


def dw_start(block, wu, wut_ref, au_ref, ad_ref):
    for c in block:
        c.wait()
    wut_ref[...] = wu[...].T
    au_ref[...] = jnp.zeros_like(au_ref)
    ad_ref[...] = jnp.zeros_like(ad_ref)


def dw_mlp_kernel(l, lr_ref, n_ref, g_ref, wu_ref, wd_ref, nu_ref, nd_ref, wut_ref, au_ref, ad_ref, wu_buf, wd_buf, sem):
    i = pl.program_id(0)

    @pl.when(i == 0)
    def _():
        block = load_block(l, lax.axis_index("sp"), wu_ref, wd_ref, wu_buf, wd_buf, sem)
        for c in block:
            c.start()
        dw_start(block, wu_buf, wut_ref, au_ref, ad_ref)

    dw_tile(wut_ref[...], wd_buf[...], n_ref[...].reshape(SEQ, D), g_ref[...].reshape(SEQ, D), au_ref, ad_ref)

    @pl.when(i == pl.num_programs(0) - 1)
    def _():
        nu_ref[...], nd_ref[...] = dw_finish(lr_ref[0], wut_ref[...], wd_buf[...], au_ref[...], ad_ref[...])


def dw_mlp(l, lr, n_all, g4, wu, wd):
    return pl.pallas_call(
        functools.partial(dw_mlp_kernel, l), grid=(NDEV,),
        in_specs=[SMEM, token_spec(n_all), token_spec(g4), ANY, ANY],
        out_specs=[full(D, FB), full(FB, D)], out_shape=[jax.ShapeDtypeStruct((D, FB), BF), jax.ShapeDtypeStruct((FB, D), BF)],
        scratch_shapes=[pltpu.VMEM((FB, D), BF), pltpu.VMEM((FB, D), F32), pltpu.VMEM((FB, D), F32),
                        pltpu.VMEM((D, FB), BF), pltpu.VMEM((FB, D), BF), pltpu.SemaphoreType.DMA((2,))],
        cost_estimate=cost(8 * NDEV * SEQ * D * FB, 24),
        name="dw_mlp",
    )(lr, n_all, g4, wu, wd)


NB = 2


def dw_chip_kernel(part, lr_ref, n_ref, g_ref, wu_ref, wd_ref, src_ref, st_ref, all_ref, wut_ref, au_ref, ad_ref, buf_ref,
                   wu_buf, wd_buf, st_s, st_r, st_l, sem, sp_s, sp_r):
    s = pl.program_id(0)
    me = lax.axis_index("sp")
    core = lax.rem(me, 2)
    partner = me + 1 - 2 * core
    x_dev = me + 2 - 4 * lax.rem(me // 2, 2)
    y_dev = me + 4 - 8 * (me // 4)

    def push(k, src, dst, dev):
        return pltpu.make_async_remote_copy(src_ref=src, dst_ref=dst, send_sem=sp_s.at[k], recv_sem=sp_r.at[k],
                                            device_id={"sp": dev}, device_id_type=MESH_ID)

    if part == 0:
        own = pltpu.make_async_copy(src_ref, all_ref.at[me], st_l.at[NB])
        spread = [push(k, src_ref, all_ref.at[me], dev) for k, dev in enumerate((x_dev, y_dev, partner))]
    else:
        lo, hi = pl.ds(0, FB // 2), pl.ds(FB // 2, FB // 2)
        far = x_dev + y_dev - me
        spread = [push(k, all_ref.at[at], all_ref.at[at], dev) for k, (at, dev) in enumerate(
            (((x_dev, lo), y_dev), ((y_dev, hi), x_dev), (x_dev, partner), (y_dev, partner)))]
        late = push(4, all_ref.at[far], all_ref.at[far], partner)

    def copies(b):
        row = core * NB + b
        return (pltpu.make_async_copy(buf_ref.at[b], st_ref.at[row], st_l.at[b]),
                pltpu.make_async_remote_copy(src_ref=buf_ref.at[b], dst_ref=st_ref.at[row], send_sem=st_s.at[b],
                                             recv_sem=st_r.at[b], device_id={"sp": partner}, device_id_type=MESH_ID))

    blocks = [load_block(0, (core * 2 + part) * NB + b, wu_ref, wd_ref, wu_buf.at[b], wd_buf.at[b], sem.at[b])
              for b in range(NB)]

    @pl.when(s == 0)
    def _():
        for block in blocks:
            for c in block:
                c.start()
        barrier = pltpu.get_barrier_semaphore()
        for dev in (x_dev, y_dev, partner):
            pl.semaphore_signal(barrier, inc=1, device_id={"sp": dev}, device_id_type=MESH_ID)
        pl.semaphore_wait(barrier, 3)
        if part == 0:
            own.start()
        for c in spread:
            c.start()

    if part == 1:
        @pl.when(s == 12)
        def _():
            spread[0].wait_recv()
            spread[1].wait_recv()
            late.start()

    for b in range(NB):
        @pl.when(s == b * NDEV)
        def _():
            dw_start(blocks[b], wu_buf.at[b], wut_ref, au_ref, ad_ref)

    @pl.when(s < NB * NDEV)
    def _():
        dw_tile(wut_ref[...], wd_buf[s // NDEV], n_ref[...].reshape(SEQ, D), g_ref[...].reshape(SEQ, D), au_ref, ad_ref)

    for b in range(NB):
        @pl.when(s == (b + 1) * NDEV - 1)
        def _():
            nu, nd = dw_finish(lr_ref[0], wut_ref[...], wd_buf[b], au_ref[...], ad_ref[...])
            buf_ref[b, 0:D] = nu
            buf_ref[b, D:D + FB] = nd[:, :FB]
            buf_ref[b, D + FB:] = nd[:, FB:]

        @pl.when(s == (b + 1) * NDEV)
        def _():
            for c in copies(b):
                c.start()

    @pl.when(s == NB * NDEV)
    def _():
        for b in range(NB):
            for c in copies(b):
                c.wait()
        if part == 0:
            for c in [own] + spread:
                c.wait()
        else:
            spread[0].wait_send()
            spread[1].wait_send()
            for c in spread[2:] + [late]:
                c.wait()


def dw_chip(part, lr, n_all, g4, wu, wd, spread):
    last = NB * NDEV - 1
    tile = lambda i: lax.rem(jnp.minimum(i, last), NDEV)
    return pl.pallas_call(
        functools.partial(dw_chip_kernel, part), grid=(NB * NDEV + 1,),
        in_specs=[SMEM, token_spec(n_all, tile), token_spec(g4, tile), ANY, ANY, ANY],
        out_specs=[ANY, ANY],
        out_shape=[jax.ShapeDtypeStruct((2 * NB, 2 * D, FB), BF), jax.ShapeDtypeStruct((NDEV, FB, D), BF)],
        input_output_aliases={5: 1} if part else {},
        scratch_shapes=[pltpu.VMEM((FB, D), BF), pltpu.VMEM((FB, D), F32), pltpu.VMEM((FB, D), F32),
                        pltpu.VMEM((NB, 2 * D, FB), BF), pltpu.VMEM((NB, D, FB), BF), pltpu.VMEM((NB, FB, D), BF)]
        + [pltpu.SemaphoreType.DMA((NB + 1,))] * 3 + [pltpu.SemaphoreType.DMA((NB, 2))] + [pltpu.SemaphoreType.DMA((NDEV,))] * 2,
        compiler_params=pltpu.CompilerParams(collective_id=12 + part, has_side_effects=True),
        cost_estimate=cost(NB * 8 * NDEV * SEQ * D * FB, 48),
        name="dw_chip",
    )(lr, n_all, g4, wu, wd, spread)


def dw_attn_kernel(l, lr_ref, n_ref, g_ref, d_ref, o_ref, wq_ref, wk_ref, wv_ref, wo_ref, w_ref, aq_ref, ao_ref, w_buf, wo_buf, sem):
    i = pl.program_id(0)
    at = pl.ds(pl.multiple_of(lax.axis_index("sp") * LANE, LANE), LANE)
    loads = [pltpu.make_async_copy(w.at[l, :, at], w_buf.at[k], sem.at[k]) for k, w in enumerate((wq_ref, wk_ref, wv_ref))]
    loads.append(pltpu.make_async_copy(wo_ref.at[l, at, :], wo_buf, sem.at[3]))

    @pl.when(i == 0)
    def _():
        for c in loads:
            c.start()
        aq_ref[...] = jnp.zeros_like(aq_ref)
        ao_ref[...] = jnp.zeros_like(ao_ref)

    aq_ref[...] += dot_nn(d_ref[...].T, n_ref[...].reshape(SEQ, D))
    ao_ref[...] += dot_nn(o_ref[...].T, g_ref[...].reshape(SEQ, D))

    @pl.when(i == pl.num_programs(0) - 1)
    def _():
        for c in loads:
            c.wait()
        lr = lr_ref[0]
        for k in range(3):
            at = slice(k * LANE, (k + 1) * LANE)
            w_ref[:, at] = (w_buf[k].astype(F32) - lr * aq_ref[at].T).astype(BF)
        no = (wo_buf[...].astype(F32) - lr * ao_ref[...]).astype(BF)
        for c in range(D // LANE):
            at = slice(c * LANE, (c + 1) * LANE)
            w_ref[at, QKV:512] = no[:, at]


def dw_attn(l, lr, n_all, g4, d_all, o_all, *weights):
    return pl.pallas_call(
        functools.partial(dw_attn_kernel, l), grid=(NDEV,),
        in_specs=[SMEM, token_spec(n_all), token_spec(g4), pl.BlockSpec((None, SEQ, QKV), lambda i: (i, 0, 0)),
                  pl.BlockSpec((None, SEQ, LANE), lambda i: (i, 0, 0))] + [ANY] * 4,
        out_specs=full(D, 512), out_shape=jax.ShapeDtypeStruct((D, 512), BF),
        scratch_shapes=[pltpu.VMEM((QKV, D), F32), pltpu.VMEM((LANE, D), F32), pltpu.VMEM((3, D, LANE), BF),
                        pltpu.VMEM((LANE, D), BF), pltpu.SemaphoreType.DMA((4,))],
        cost_estimate=cost(2 * NDEV * SEQ * D * 512, 24),
        name="dw_attn",
    )(lr, n_all, g4, d_all, o_all, *weights)


def norm_kernel(x_ref, gain_ref, n_ref):
    n_ref[...] = norm_apply(x_ref[...].astype(F32), gain_ref[...]).astype(BF)


def norm_tokens(x, gain_row):
    return pl.pallas_call(
        norm_kernel, grid=(NDEV,), in_specs=[pl.BlockSpec((SEQ, D), lambda i: (i, 0)), full(1, D)],
        out_specs=pl.BlockSpec((SEQ, D), lambda i: (i, 0)), out_shape=jax.ShapeDtypeStruct(x.shape, BF),
        cost_estimate=cost(1 << 28, 16), name="norm_tokens",
    )(x, gain_row)


def place_mlp_kernel(w_ref, *rest):
    u_ref, d_ref = rest[-2:]
    u_ref[...] = w_ref[0:D]
    d_ref[:, :FB] = w_ref[D:D + FB]
    d_ref[:, FB:] = w_ref[D + FB:]


def place_mlp(l, layers, w_all, prev, column):
    prev = list(prev)
    ff = NDEV * FB
    return pl.pallas_call(
        place_mlp_kernel, grid=(w_all.shape[0] // (2 * D),),
        in_specs=[pl.BlockSpec((2 * D, FB), lambda i: (i, 0))] + [ANY] * len(prev),
        out_specs=[pl.BlockSpec((None, D, FB), lambda i: (l, 0, column(i))), pl.BlockSpec((None, FB, D), lambda i: (l, column(i), 0))],
        out_shape=[jax.ShapeDtypeStruct((layers, D, ff), BF), jax.ShapeDtypeStruct((layers, ff, D), BF)],
        input_output_aliases={1 + i: i for i in range(len(prev))},
        cost_estimate=cost(1 << 30, 32),
        name="place_mlp",
    )(w_all, *prev)


def place_kernel(w_ref, prev_ref, o_ref):
    o_ref[...] = w_ref[...]


def place_up(l, w_all, prev):
    return pl.pallas_call(
        place_kernel, grid=(NDEV,), in_specs=[pl.BlockSpec((D, FB), lambda i: (i, 0)), ANY],
        out_specs=pl.BlockSpec((None, D, FB), lambda i: (l, 0, i)), out_shape=jax.ShapeDtypeStruct(prev.shape, BF),
        input_output_aliases={1: 0}, cost_estimate=cost(1 << 29, 16), name="place_up",
    )(w_all, prev)


def place_down(l, w_all, prev):
    return pl.pallas_call(
        place_kernel, grid=(NDEV,), in_specs=[pl.BlockSpec((FB, D), lambda i: (i, 0)), ANY],
        out_specs=pl.BlockSpec((None, FB, D), lambda i: (l, i, 0)), out_shape=jax.ShapeDtypeStruct(prev.shape, BF),
        input_output_aliases={1: 0}, cost_estimate=cost(1 << 29, 16), name="place_down",
    )(w_all, prev)


def place_attn_kernel(w_ref, *rest):
    q_ref, k_ref, v_ref, o_ref = rest[-4:]
    q_ref[...] = w_ref[:, 0:LANE]
    k_ref[...] = w_ref[:, LANE:256]
    v_ref[...] = w_ref[:, 256:QKV]
    for c in range(D // LANE):
        o_ref[:, c * LANE:(c + 1) * LANE] = w_ref[c * LANE:(c + 1) * LANE, QKV:512]


def place_attn(l, layers, w_all, prev):
    prev = list(prev)
    col = pl.BlockSpec((None, D, LANE), lambda i: (l, 0, i))
    return pl.pallas_call(
        place_attn_kernel, grid=(NDEV,),
        in_specs=[pl.BlockSpec((D, 512), lambda i: (i, 0))] + [ANY] * len(prev),
        out_specs=[col, col, col, pl.BlockSpec((None, LANE, D), lambda i: (l, i, 0))],
        out_shape=[jax.ShapeDtypeStruct((layers, D, D), BF)] * 4,
        input_output_aliases={1 + i: i for i in range(len(prev))},
        cost_estimate=cost(1 << 30, 16),
        name="place_attn",
    )(w_all, *prev)


def solution(mesh):
    act_spec = P("dp", "sp", None)
    out_four = P("dp", None, None, None)
    out_three = P("dp", None, None)

    def step(hidden_in, positions, grad_y, w_query, w_key, w_value, w_out, w_up, w_down, gain, learn_rate):
        layers = w_query.shape[0]
        idx = lax.axis_index("sp")
        chunk = SEQ // NDEV
        lr = learn_rate.reshape(1)

        def gather(t):
            return lax.all_gather(t, "sp", axis=0, tiled=True)

        def swap(t):
            return lax.all_to_all(t, "sp", 0, 0, tiled=True)

        def own(t):
            return lax.dynamic_index_in_dim(t, idx, 1, keepdims=False).reshape(SEQ, D)

        pos_tile = jnp.zeros((8, LANE), jnp.int32).at[0, :chunk].set(positions)
        pos = share(jnp.broadcast_to(pos_tile, (NDEV, 8, LANE)))[:, 0, :chunk].reshape(SEQ)

        x_all = lax.all_gather(hidden_in, "sp", axis=0, tiled=False)
        gy_all = lax.all_gather(grad_y, "sp", axis=0, tiled=False)
        lane = jnp.arange(LANE, dtype=jnp.int32)
        freqs = ROPE_BASE ** (-(lane % (HD // 2)).astype(F32) / (HD // 2))
        angles = pos.astype(F32)[:, None] * freqs[None, :]
        c_tab = jnp.cos(angles)
        s_tab = jnp.sin(angles) * jnp.where(lane % HD < HD // 2, -1.0, 1.0)[None, :]

        wq = w_query.reshape(layers, D, D)
        wk = w_key.reshape(layers, D, D)
        wv = w_value.reshape(layers, D, D)
        wo = w_out.reshape(layers, D, D)

        def gain_row(l):
            return gain[l].reshape(1, D)

        x0 = own(x_all)
        n0 = norm_apply(x0.astype(F32), gain[0]).astype(BF)
        q0, k0, v0, o0, o_pack0, lse0 = attn_fwd(0, n0, wq, wk, wv, c_tab, s_tab)
        o_all0 = swap(o_pack0)
        pre0, x1, n1 = mlp_fwd(0, False, n0, x0, o0, wo, w_up, w_down, gain_row(1))
        n1_all = gather(n1).reshape(1, NDEV, SEQ, D)
        q1, k1, v1, o1, o_pack1, lse1 = attn_fwd(1, n1, wq, wk, wv, c_tab, s_tab)
        o_all1 = swap(o_pack1)
        pre1, y = mlp_fwd(1, True, n1, x1, o1, wo, w_up, w_down, gain_row(1))
        out_y = swap(y.reshape(NDEV, chunk, D))

        gy = own(gy_all)
        dn1, d_pack1 = attn_bwd(1, gy, wo, wq, wk, wv, q1, k1, v1, lse1, c_tab, s_tab)
        d_all1 = swap(d_pack1)
        g0 = mlp_bwd(1, gy, pre1, w_up, w_down, dn1, x1, gain_row(1))
        g0_all = gather(g0).reshape(1, NDEV, SEQ, D)
        tie = lax.optimization_barrier

        dn0, d_pack0 = attn_bwd(0, g0, wo, wq, wk, wv, q0, k0, v0, lse0, c_tab, s_tab)
        d_all0 = swap(d_pack0)
        d_all1, dn0 = tie((d_all1, dn0))
        w_attn1 = dw_attn(1, lr, n1_all, gy_all, d_all1, o_all1, wq, wk, wv, wo)
        w_attn1_all = gather(w_attn1)
        dn0, w_attn1 = tie((dn0, w_attn1))
        gx = mlp_bwd(0, g0, pre0, w_up, w_down, dn0, x0, gain_row(0))
        grad_x = swap(gx.reshape(NDEV, chunk, D))
        gy_all, gx = tie((gy_all, gx))
        w_up1, w_mlp1 = dw_mlp(1, lr, n1_all, gy_all, w_up, w_down)
        w_up1_all = gather(w_up1)
        x_all, w_mlp1 = tie((x_all, w_mlp1))
        n0_all = norm_tokens(x_all.reshape(NDEV * SEQ, D), gain_row(0)).reshape(x_all.shape)
        w_attn0 = dw_attn(0, lr, n0_all, g0_all, d_all0, o_all0, wq, wk, wv, wo)
        w_attn0_all = gather(w_attn0)
        n0_all, w_attn0 = tie((n0_all, w_attn0))
        st0, w_down1 = dw_chip(0, lr, n0_all, g0_all, w_up, w_down, w_mlp1)
        n0_all, st0 = tie((n0_all, st0))
        st1, w_down1 = dw_chip(1, lr, n0_all, g0_all, w_up, w_down, w_down1)
        up_down = ()
        for a, st in enumerate((st0, st1)):
            up_down = place_mlp(0, layers, st.reshape(2 * NB * 2 * D, FB), up_down,
                                lambda i, a=a: (i // NB) * 2 * NB + a * NB + lax.rem(i, NB))
        attn_new = place_attn(1, layers, w_attn1_all, ())
        attn_new = place_attn(0, layers, w_attn0_all, attn_new)
        new_down = place_down(1, w_down1.reshape(NDEV * FB, D), up_down[1])
        new_up = place_up(1, w_up1_all, up_down[0])
        nq, nk, nv, no = attn_new
        return (out_y, grad_x, nq.reshape(w_query.shape), nk.reshape(w_query.shape), nv.reshape(w_query.shape),
                no.reshape(w_out.shape), new_up, new_down)

    return jax.shard_map(step, mesh=mesh,
                         in_specs=(act_spec, P(("dp", "sp")), act_spec, P(), P(), P(), P(), P(), P(), P(), P()),
                         out_specs=(act_spec, act_spec, out_four, out_four, out_four, out_four, out_three, out_three),
                         check_vma=False)
```

time: 654 us -> 615 us (0.940)
  waiting for transfers between devices: 171 us -> 39.2 us
  blocking collectives: 0 us -> 106 us
  Pallas kernels: 396 us -> 381 us
  starting transfers between devices: 0.49 us -> 12.4 us
  local copies, waits for them, and re-layouts: 54.7 us -> 46.3 us
    all_gather x7 -> x5, waiting for transfers between devices: 168 us -> 0.03 us  [gather(): return lax.all_gather(t, 'sp', axis=0, tiled=True)]
    all_to_all x0 -> x3, blocking collectives: none -> 106 us  [swap(): return lax.all_to_all(t, 'sp', 0, 0, tiled=True)]
    all_gather x0 -> x1, waiting for transfers between devices: none -> 22.4 us  [step(): x_all = lax.all_gather(hidden_in, 'sp', axis=0, tiled=False)]
    pallas_call x15 -> x19, Pallas kernels: 377 us -> 363 us  [the longest x2 106 us: dw_chip(): pl.pallas_call(functools.partial(dw_chip_kernel, part), grid=(NB * NDEV +...]
    all_gather x1, waiting for transfers between devices: 0.02 us -> 13.1 us  [step(): gy_all = lax.all_gather(grad_y, 'sp', axis=0, tiled=False)]
    all_to_all x0 -> x3, starting transfers between devices: none -> 12.1 us  [swap(): return lax.all_to_all(t, 'sp', 0, 0, tiled=True)]
    squeeze x3 -> x0, local copies, waits for them, and re-layouts: 7.91 us -> none  [the longest x1 3.03 us: step(): wd_s = lax.dynamic_slice(w_down, (l, idx * FB, 0), (1, FB, D))[0]]
  transfers between devices with their start and end apart: 8 -> 10, of which waited for: 3 -> 3; matrix products, arithmetic and copies ran while one was open for 9% -> 8% of each run, Pallas kernels for 59% -> 62%
where the time goes in v2:
time: 615 us; the launch traced here: 605 us
  Pallas kernels  381 us (62%)
  blocking collectives  106 us (17%)
  local copies, waits for them, and re-layouts  46.3 us (8%)
  waiting for transfers between devices  39.2 us (6%)
  between operations  15.1 us (2%)
  starting transfers between devices  12.4 us (2%)
    pallas_call x2, Pallas kernels, dw_chip(): pl.pallas_call(functools.partial(dw_chip_kernel, part), grid=(NB * NDEV +...  106 us
    all_to_all x3, blocking collectives, swap(): return lax.all_to_all(t, 'sp', 0, 0, tiled=True)  106 us
    pallas_call x2, Pallas kernels, attn_bwd(): pl.pallas_call(attn_bwd_kernel, grid=(nb,), in_specs=[full(SEQ, D), pl.Bl...  51.2 us
    pallas_call x2, Pallas kernels, mlp_bwd(): pl.pallas_call(mlp_bwd_kernel, grid=(ff // MB,), in_specs=[full(SEQ, D),...  37.6 us
    pallas_call x2, Pallas kernels, mlp_fwd(): pl.pallas_call(functools.partial(mlp_fwd_kernel, last), grid=(ff // MB,),...  34.7 us
    pallas_call x2, Pallas kernels, attn_fwd(): pl.pallas_call(attn_fwd_kernel, grid=(nb,), in_specs=[full(SEQ, D), wspec...  33.2 us
    pallas_call x1, Pallas kernels, dw_mlp(): pl.pallas_call(functools.partial(dw_mlp_kernel, l), grid=(NDEV,), in_spec...  25.5 us
    pallas_call x2, Pallas kernels, dw_attn(): pl.pallas_call(functools.partial(dw_attn_kernel, l), grid=(NDEV,), in_spe...  25.5 us
  transfers between devices with their start and end apart: 10, of which 3 were waited for; matrix products, arithmetic and copies ran while one was open for 8% of the time, Pallas kernels for 62%

profile of v2, /device:TPU:1, one launch (start us, length us, event | category | flops | bytes accessed | tf_op | source)
XLA Modules:
  0.0 605.4 jit_solution(532308070516709512)
XLA Ops:
  10.0 6.3 %share.1 = s32[8,8,128]{2,1,0:T(8,128)} custom-call(s32[8,8,128]{2,1,0:T(8,128)} %broadcast_in_dim.16.p_ref), custom_call_target="tpu_custom_call" | custom-call | tf_op jit(solution)/shard_map/share/pallas_call | solution.py:250
  17.1 6.2 %copy.55.wq_ref = bf16[2,1024,1024]{2,1,0:T(8,128)(2,1)} copy(bf16[2,1024,1024]{1,2,0:T(8,128)(2,1)} %bitcast.56) | data formatting | bytes 8388608 | tf_op jit(solution)/shard_map/reshape | solution.py:673
  23.4 6.2 %copy.56.wk_ref = bf16[2,1024,1024]{2,1,0:T(8,128)(2,1)} copy(bf16[2,1024,1024]{1,2,0:T(8,128)(2,1)} %bitcast.57) | data formatting | bytes 8388608 | tf_op jit(solution)/shard_map/reshape | solution.py:674
  29.5 6.3 %copy.57.wv_ref = bf16[2,1024,1024]{2,1,0:T(8,128)(2,1)} copy(bf16[2,1024,1024]{1,2,0:T(8,128)(2,1)} %bitcast.58) | data formatting | bytes 8388608 | tf_op jit(solution)/shard_map/reshape | solution.py:675
  38.3 22.4 %all-gather.20.cloned.1.call-done = bf16[64,64,1024]{2,1,0:T(8,128)(2,1)} async-done(((bf16[8,64,1024]{2,1,0:T(8,128)(2,1)}), bf16[64,64,1024]{2,1,0:T(8,128)(2,1)}) %all-gather.20.cloned.1.call-update) | async-done | bytes 8388624 | tf_op jit(solution)/shard_map/all_gather | solution.py:665
  63.6 16.6 %attn_fwd.2 = (bf16[512,1024]{1,0:T(8,128)(2,1)}, bf16[512,1024]{1,0:T(8,128)(2,1)}, bf16[512,1024]{1,0:T(8,128)(2,1)}, bf16[512,1024]{1,0:T(8,128)(2,1)}, bf16[...) custom-call(bf16[512,1024]{1,0:T(8,128)(2,1)} %multiply_convert_fusion.n_ref, bf16[2,1024,1024]{2,1,0:T(8,128)(2,1)} %copy.55.wq_ref, ...), custom_call_target="tpu_custom_call" | custom-call | flops 5368709120 | bytes 14680064 | tf_op jit(solution)/shard_map/attn_fwd/pallas_call | solution.py:105
  80.2 17.7 %mlp_fwd.2 = (f32[512,4096]{1,0:T(8,128)}, bf16[512,1024]{1,0:T(8,128)(2,1)}, bf16[512,1024]{1,0:T(8,128)(2,1)}) custom-call(bf16[512,1024]{1,0:T(8,128)(2,1)} %multiply_convert_fusion.n_ref, bf16[512,1024]{1,0:T(8,128)(2,1)} %bitcast.39, bf16[512,1024]{1,0:T(8,128)(2,1)} %get-tuple-element.68.o_ref, bf16[2,1024,1024]{2,1,0:T(8,128)(2,1)} %bitcast.30, ...), custom_call_target="tpu_custom_call" | custom-call | flops 9663676416 | bytes 31457280 | tf_op jit(solution)/shard_map/mlp_fwd/pallas_call | solution.py:305
  98.2 13.1 %all-gather.22.cloned.1.call-done = bf16[64,64,1024]{2,1,0:T(8,128)(2,1)} async-done(((bf16[8,64,1024]{2,1,0:T(8,128)(2,1)}), bf16[64,64,1024]{2,1,0:T(8,128)(2,1)}) %all-gather.22.cloned.1.call-update) | async-done | bytes 8388624 | tf_op jit(solution)/shard_map/all_gather | solution.py:666
  113.6 16.6 %attn_fwd.3 = (bf16[512,1024]{1,0:T(8,128)(2,1)}, bf16[512,1024]{1,0:T(8,128)(2,1)}, bf16[512,1024]{1,0:T(8,128)(2,1)}, bf16[512,1024]{1,0:T(8,128)(2,1)}, bf16[...) custom-call(bf16[512,1024]{1,0:T(8,128)(2,1)} %get-tuple-element.69.n_ref, bf16[2,1024,1024]{2,1,0:T(8,128)(2,1)} %copy.55.wq_ref, ...), custom_call_target="tpu_custom_call" | custom-call | flops 5368709120 | bytes 14680064 | tf_op jit(solution)/shard_map/attn_fwd/pallas_call | solution.py:105
  130.2 17.0 %mlp_fwd.3 = (f32[512,4096]{1,0:T(8,128)}, bf16[512,1024]{1,0:T(8,128)(2,1)}) custom-call(bf16[512,1024]{1,0:T(8,128)(2,1)} %get-tuple-element.69.n_ref, bf16[512,1024]{1,0:T(8,128)(2,1)} %get-tuple-element.70.x_ref, bf16[512,1024]{1,0:T(8,128)(2,1)} %get-tuple-element.71.o_ref, bf16[2,1024,1024]{2,1,0:T(8,128)(2,1)} %bitcast.31, ...), custom_call_target="tpu_custom_call" | custom-call | flops 9663676416 | bytes 31457280 | tf_op jit(solution)/shard_map/mlp_fwd/pallas_call | solution.py:305
  147.2 25.6 %attn_bwd.2 = (f32[512,1024]{1,0:T(8,128)}, bf16[8,512,384]{2,1,0:T(8,128)(2,1)}) custom-call(bf16[512,1024]{1,0:T(8,128)(2,1)} %bitcast.54, bf16[2,1024,1024]{2,1,0:T(8,128)(2,1)} %bitcast.32, bf16[2,1024,1024]{2,1,0:T(8,128)(2,1)} %copy.55.wq_ref, bf16[2,1024,1024]{2,1,0:T(8,128)(2,1)} %copy.56.wk_ref, bf16[2,1024,1024]{2,1,0:T(8,128)(2,1)} %copy.57.wv_ref, ...), custom_call_target="tpu_custom_call" | custom-call | flops 9663676416 | bytes 20971520 | tf_op jit(solution)/shard_map/attn_bwd/pallas_call | solution.py:188
  172.9 18.1 %mlp_bwd.2.g_ref = bf16[512,1024]{1,0:T(8,128)(2,1)} custom-call(bf16[512,1024]{1,0:T(8,128)(2,1)} %bitcast.55, f32[512,4096]{1,0:T(8,128)} %get-tuple-element.73.pre_ref, bf16[2,1024,4096]{2,1,0:T(8,128)(2,1)} %wu_ref.13, bf16[2,4096,1024]{2,1,0:T(8,128)(2,1)} %wd_ref.13, f32[512,1024]{1,0:T(8,128)} %get-tuple-element.78.dn_ref, ...), custom_call_target="tpu_custom_call" | custom-call | flops 8589934592 | bytes 31457280 | tf_op jit(solution)/shard_map/mlp_bwd/pallas_call | solution.py:340
  191.0 51.8 %all_to_all.30.d_ref = bf16[8,512,384]{2,1,0:T(8,128)(2,1)} all-to-all(bf16[8,512,384]{2,1,0:T(8,128)(2,1)S(1)} %copy-done.3), channel_id=1, replica_groups=mesh['dp'=1,'sp'=8] {'sp'}, dimensions={0} | all-to-all | bytes 6291456 | tf_op jit(solution)/shard_map/all_to_all | solution.py:657
  248.3 25.6 %attn_bwd.3 = (f32[512,1024]{1,0:T(8,128)}, bf16[8,512,384]{2,1,0:T(8,128)(2,1)}) custom-call(bf16[512,1024]{1,0:T(8,128)(2,1)} %mlp_bwd.2.g_ref, bf16[2,1024,1024]{2,1,0:T(8,128)(2,1)} %bitcast.33, bf16[2,1024,1024]{2,1,0:T(8,128)(2,1)} %copy.55.wq_ref, bf16[2,1024,1024]{2,1,0:T(8,128)(2,1)} %copy.56.wk_ref, bf16[2,1024,1024]{2,1,0:T(8,128)(2,1)} %copy.57.wv_ref, ...), custom_call_target="tpu_custom_call" | custom-call | flops 9663676416 | bytes 20971520 | tf_op jit(solution)/shard_map/attn_bwd/pallas_call | solution.py:188
  274.9 12.8 %dw_attn.2 = bf16[1024,512]{1,0:T(8,128)(2,1)} custom-call(f32[1]{0:T(128)} %bitcast.25.lr_ref, bf16[1,8,512,1024]{3,2,1,0:T(8,128)(2,1)} %bitcast.49, bf16[8,8,64,1024]{3,2,1,0:T(8,128)(2,1)} %bitcast.42, bf16[8,512,384]{2,1,0:T(8,128)(2,1)} %all_to_all.30.d_ref, bf16[8,512,128]{2,1,0:T(8,128)(2,1)} %copy-done.2, bf16[2,1024,1024]{2,1,0:T(8,128)(2,1)} %copy.55.wq_ref, ...), custom_call_target="tpu_custom_call" | custom-call | flops 4294967296 | bytes 25165824 | tf_op jit(solution)/shard_map/dw_attn/pallas_call | solution.py:554
  287.7 23.9 %all_to_all.31.o_ref = bf16[8,512,128]{2,1,0:T(8,128)(2,1)} all-to-all(bf16[8,512,128]{2,1,0:T(8,128)(2,1)S(1)} %copy-done.4), channel_id=1, replica_groups=mesh['dp'=1,'sp'=8] {'sp'}, dimensions={0} | all-to-all | bytes 2097152 | tf_op jit(solution)/shard_map/all_to_all | solution.py:657
  316.6 19.5 %mlp_bwd.3 = bf16[512,1024]{1,0:T(8,128)(2,1)} custom-call(bf16[512,1024]{1,0:T(8,128)(2,1)} %mlp_bwd.2.g_ref, f32[512,4096]{1,0:T(8,128)} %get-tuple-element.79.pre_ref, bf16[2,1024,4096]{2,1,0:T(8,128)(2,1)} %wu_ref.13, bf16[2,4096,1024]{2,1,0:T(8,128)(2,1)} %wd_ref.13, f32[512,1024]{1,0:T(8,128)} %get-tuple-element.89.dn_ref, bf16[512,1024]{1,0:T(8,128)(2,1)} %bitcast.40, ...), custom_call_target="tpu_custom_call" | custom-call | flops 8589934592 | bytes 31457280 | tf_op jit(solution)/shard_map/mlp_bwd/pallas_call | solution.py:340
  336.1 25.5 %dw_mlp.1 = (bf16[1024,512]{1,0:T(8,128)(2,1)}, bf16[512,1024]{1,0:T(8,128)(2,1)}) custom-call(f32[1]{0:T(128)} %bitcast.26.lr_ref, bf16[1,8,512,1024]{3,2,1,0:T(8,128)(2,1)} %bitcast.50, bf16[8,8,64,1024]{3,2,1,0:T(8,128)(2,1)} %bitcast.43, bf16[2,1024,4096]{2,1,0:T(8,128)(2,1)} %wu_ref.13, bf16[2,4096,1024]{2,1,0:T(8,128)(2,1)} %wd_ref.13), custom_call_target="tpu_custom_call" | custom-call | flops 17179869184 | bytes 25165824 | tf_op jit(solution)/shard_map/dw_mlp/pallas_call | solution.py:401
  361.6 10.3 %norm_tokens.1 = bf16[4096,1024]{1,0:T(8,128)(2,1)} custom-call(bf16[4096,1024]{1,0:T(8,128)(2,1)} %bitcast.45, f32[1,1024]{1,0:T(1,128)} %copy-done.5), custom_call_target="tpu_custom_call" | custom-call | flops 268435456 | bytes 16777216 | tf_op jit(solution)/shard_map/norm_tokens/pallas_call | solution.py:571
  375.0 12.7 %dw_attn.3 = bf16[1024,512]{1,0:T(8,128)(2,1)} custom-call(f32[1]{0:T(128)} %bitcast.27.lr_ref, bf16[8,8,64,1024]{3,2,1,0:T(8,128)(2,1)} %bitcast.36, bf16[1,8,512,1024]{3,2,1,0:T(8,128)(2,1)} %bitcast.46, bf16[8,512,384]{2,1,0:T(8,128)(2,1)} %copy-done.1, bf16[8,512,128]{2,1,0:T(8,128)(2,1)} %all_to_all.31.o_ref, bf16[2,1024,1024]{2,1,0:T(8,128)(2,1)} %copy.55.wq_ref, ...), custom_call_target="tpu_custom_call" | custom-call | flops 4294967296 | bytes 25165824 | tf_op jit(solution)/shard_map/dw_attn/pallas_call | solution.py:554
  388.5 29.8 %all_to_all.32 = bf16[8,64,1024]{2,1,0:T(8,128)(2,1)S(1)} all-to-all(bf16[8,64,1024]{2,1,0:T(8,128)(2,1)} %bitcast.63), channel_id=1, replica_groups=mesh['dp'=1,'sp'=8] {'sp'}, dimensions={0} | all-to-all | bytes 2097152 | tf_op jit(solution)/shard_map/all_to_all | solution.py:657
  418.3 53.9 %dw_chip.2 = (bf16[4,2048,512]{2,1,0:T(8,128)(2,1)}, bf16[8,512,1024]{2,1,0:T(8,128)(2,1)}) custom-call(f32[1]{0:T(128)} %bitcast.28.lr_ref, bf16[8,8,64,1024]{3,2,1,0:T(8,128)(2,1)} %bitcast.37, bf16[1,8,512,1024]{3,2,1,0:T(8,128)(2,1)} %bitcast.47, bf16[2,1024,4096]{2,1,0:T(8,128)(2,1)} %wu_ref.13, bf16[2,4096,1024]{2,1,0:T(8,128)(2,1)} %wd_ref.13, ...), custom_call_target="tpu_custom_call" | custom-call | flops 34359738368 | bytes 50331648 | tf_op jit(solution)/shard_map/dw_chip/pallas_call | solution.py:508
  474.5 52.3 %dw_chip.3 = (bf16[4,2048,512]{2,1,0:T(8,128)(2,1)}, bf16[8,512,1024]{2,1,0:T(8,128)(2,1)}) custom-call(f32[1]{0:T(128)} %bitcast.29.lr_ref, bf16[8,8,64,1024]{3,2,1,0:T(8,128)(2,1)} %bitcast.38, bf16[1,8,512,1024]{3,2,1,0:T(8,128)(2,1)} %bitcast.48, bf16[2,1024,4096]{2,1,0:T(8,128)(2,1)} %wu_ref.13, ...), custom_call_target="tpu_custom_call", output_to_operand_aliasing={{1}: (5, {})} | custom-call | flops 34359738368 | bytes 50331648 | tf_op jit(solution)/shard_map/dw_chip/pallas_call | solution.py:508
  526.8 7.2 %place_mlp.2 = (bf16[2,1024,4096]{2,1,0:T(8,128)(2,1)}, bf16[2,4096,1024]{2,1,0:T(8,128)(2,1)}) custom-call(bf16[8192,512]{1,0:T(8,128)(2,1)} %bitcast.53), custom_call_target="tpu_custom_call" | custom-call | flops 1073741824 | bytes 33554432 | tf_op jit(solution)/shard_map/place_mlp/pallas_call | solution.py:588
  534.0 7.2 %place_mlp.3 = (bf16[2,1024,4096]{2,1,0:T(8,128)(2,1)}, bf16[2,4096,1024]{2,1,0:T(8,128)(2,1)}) custom-call(bf16[8192,512]{1,0:T(8,128)(2,1)} %bitcast.52, bf16[2,1024,4096]{2,1,0:T(8,128)(2,1)} %get-tuple-element.111.rest_0_, bf16[2,4096,1024]{2,1,0:T(8,128)(2,1)} %get-tuple-element.112.rest_1_), custom_call_target="tpu_custom_call", output_to_operand_aliasing={{0}: (1, {}), {1}: (2, {})} | custom-call | flops 1073741824 | bytes 33554432 | tf_op jit(solution)/shard_map/place_mlp/pallas_call | solution.py:588
  541.1 8.9 %place_down.1 = bf16[2,4096,1024]{2,1,0:T(8,128)(2,1)} custom-call(bf16[4096,1024]{1,0:T(8,128)(2,1)} %bitcast.51, bf16[2,4096,1024]{2,1,0:T(8,128)(2,1)} %get-tuple-element.115.prev_ref), custom_call_target="tpu_custom_call", output_to_operand_aliasing={{}: (1, {})} | custom-call | flops 536870912 | bytes 16777216 | tf_op jit(solution)/shard_map/place_down/pallas_call | solution.py:612
  550.1 9.4 %place_attn.2 = (bf16[2,1024,1024]{2,1,0:T(8,128)(2,1)}, bf16[2,1024,1024]{2,1,0:T(8,128)(2,1)}, bf16[2,1024,1024]{2,1,0:T(8,128)(2,1)}, bf16[2,1024,1024]{2,1,0:T(8,128)(2,1)}) custom-call(bf16[8192,512]{1,0:T(8,128)(2,1)} %all-gather.16.cloned.1.call-done.w_ref), custom_call_target="tpu_custom_call" | custom-call | flops 1073741824 | bytes 16777216 | tf_op jit(solution)/shard_map/place_attn/pallas_call | solution.py:631
  559.5 9.4 %place_attn.3 = (bf16[2,1024,1024]{2,1,0:T(8,128)(2,1)}, bf16[2,1024,1024]{2,1,0:T(8,128)(2,1)}, bf16[2,1024,1024]{2,1,0:T(8,128)(2,1)}, bf16[2,1024,1024]{2,1,0:T(8,128)(2,1)}) custom-call(bf16[8192,512]{1,0:T(8,128)(2,1)} %all-gather.14.cloned.1.call-done.w_ref, ...), custom_call_target="tpu_custom_call", output_to_operand_aliasing={{0}: (1, {}), {1}: (2, {}), {2}: (3, {}), {3}: (4, {})} | custom-call | flops 1073741824 | bytes 16777216 | tf_op jit(solution)/shard_map/place_attn/pallas_call | solution.py:631
  568.9 6.2 %copy.73 = bf16[2,1024,1024]{1,2,0:T(8,128)(2,1)} copy(bf16[2,1024,1024]{2,1,0:T(8,128)(2,1)} %get-tuple-element.99) | data formatting | bytes 8388608 | tf_op jit(solution)/shard_map/place_attn/pallas_call | solution.py:631
  575.1 6.2 %copy.74 = bf16[2,1024,1024]{1,2,0:T(8,128)(2,1)} copy(bf16[2,1024,1024]{2,1,0:T(8,128)(2,1)} %get-tuple-element.100) | data formatting | bytes 8388608 | tf_op jit(solution)/shard_map/place_attn/pallas_call | solution.py:631
  581.3 6.2 %copy.75 = bf16[2,1024,1024]{1,2,0:T(8,128)(2,1)} copy(bf16[2,1024,1024]{2,1,0:T(8,128)(2,1)} %get-tuple-element.101) | data formatting | bytes 8388608 | tf_op jit(solution)/shard_map/place_attn/pallas_call | solution.py:631
  587.5 8.9 %place_up.1 = bf16[2,1024,4096]{2,1,0:T(8,128)(2,1)} custom-call(bf16[8192,512]{1,0:T(8,128)(2,1)} %all-gather.18.cloned.1.call-done.w_ref, bf16[2,1024,4096]{2,1,0:T(8,128)(2,1)} %get-tuple-element.113.prev_ref), custom_call_target="tpu_custom_call", output_to_operand_aliasing={{}: (1, {})} | custom-call | flops 536870912 | bytes 16777216 | tf_op jit(solution)/shard_map/place_up/pallas_call | solution.py:604
  (53 shorter events, 30.4 us)
Async XLA Ops:
  7.2 53.6 %all-gather.20.cloned.1.call-start = ((), (), s32[]{:S(2)}) async-start(), calls=%async_computation.11 | async-start | bytes 9437184 | tf_op jit(solution)/shard_map/all_gather | solution.py:665
  7.9 103.4 %all-gather.22.cloned.1.call-start = ((), (), s32[]{:S(2)}) async-start(), calls=%async_computation.12 | async-start | bytes 9437184 | tf_op jit(solution)/shard_map/all_gather | solution.py:666
  8.7 265.2 %all-gather.10.cloned.1.call-start = ((), (), s32[]{:S(2)}) async-start(), calls=%async_computation.6 | async-start | bytes 9437184 | tf_op jit(solution)/shard_map/all_gather | solution.py:654
  29.5 6.4 %copy-start.6 = (f32[2,1024]{1,0:T(2,128)S(1)}, f32[2,1024]{1,0:T(2,128)}, u32[]{:S(2)}) copy-start(f32[2,1024]{1,0:T(2,128)} %param.22) | copy-start | bytes 24580
  36.5 43.7 %copy-start.5 = (f32[1,1024]{1,0:T(1,128)}, f32[1,1024]{1,0:T(1,128)S(1)}, u32[]{:S(2)}) copy-start(f32[1,1024]{1,0:T(1,128)S(1)} %get-tuple-element.127.gain_ref) | copy-start | bytes 12292
  62.2 18.0 %copy-start = (bf16[8,1,64,1024]{3,2,1,0:T(8,128)(2,1)}, bf16[8,1,64,1024]{3,2,1,0:T(8,128)(2,1)S(1)}, u32[]{:S(2)}) copy-start(bf16[8,1,64,1024]{3,2,1,0:T(8,128)(2,1)S(1)} %get-tuple-element.125) | copy-start | bytes 3145732
  98.0 275.4 %all-gather.12.cloned.1.call-start = ((), (), s32[]{:S(2)}) async-start(), calls=%async_computation.7 | async-start | bytes 9437184 | tf_op jit(solution)/shard_map/all_gather | solution.py:654
  172.9 18.1 %copy-start.3 = (bf16[8,512,384]{2,1,0:T(8,128)(2,1)S(1)}, bf16[8,512,384]{2,1,0:T(8,128)(2,1)}, u32[]{:S(2)}) copy-start(bf16[8,512,384]{2,1,0:T(8,128)(2,1)} %get-tuple-element.80) | copy-start | bytes 9437188
  242.8 31.0 %all-to-all-start.2 = ((bf16[8,512,128]{2,1,0:T(8,128)(2,1)}), bf16[8,512,128]{2,1,0:T(8,128)(2,1)S(1)}, u32[]{:S(2)}, u32[]{:S(2)}) async-start(bf16[8,512,128]{2,1,0:T(8,128)(2,1)} %get-tuple-element.88), calls=%async_computation.2 | async-start | bytes 2097152 | tf_op jit(solution)/shard_map/all_to_all | solution.py:657
  247.6 302.4 %all-gather.16.cloned.1.call-start = ((), (), s32[]{:S(2)}) async-start(), calls=%async_computation.9 | async-start | bytes 9437184 | tf_op jit(solution)/shard_map/all_gather | solution.py:654
  273.9 1.0 copy-start.2
  274.9 12.8 %copy-start.4 = (bf16[8,512,128]{2,1,0:T(8,128)(2,1)S(1)}, bf16[8,512,128]{2,1,0:T(8,128)(2,1)}, u32[]{:S(2)}) copy-start(bf16[8,512,128]{2,1,0:T(8,128)(2,1)} %get-tuple-element.94) | copy-start | bytes 3145732
  311.6 61.7 %all-to-all-start.4 = ((bf16[8,512,384]{2,1,0:T(8,128)(2,1)}), bf16[8,512,384]{2,1,0:T(8,128)(2,1)S(1)}, u32[]{:S(2)}, u32[]{:S(2)}) async-start(bf16[8,512,384]{2,1,0:T(8,128)(2,1)} %get-tuple-element.93), calls=%async_computation.4 | async-start | bytes 6291456 | tf_op jit(solution)/shard_map/all_to_all | solution.py:657
  316.6 242.9 %all-gather.14.cloned.1.call-start = ((), (), s32[]{:S(2)}) async-start(), calls=%async_computation.8 | async-start | bytes 9437184 | tf_op jit(solution)/shard_map/all_gather | solution.py:654
  373.4 1.7 copy-start.1
  387.7 199.8 %all-gather.18.cloned.1.call-start = ((), (), s32[]{:S(2)}) async-start(), calls=%async_computation.10 | async-start | bytes 9437184 | tf_op jit(solution)/shard_map/all_gather | solution.py:654
  472.2 77.9 %all-to-all-start.3 = ((bf16[8,64,1024]{2,1,0:T(8,128)(2,1)}), bf16[8,64,1024]{2,1,0:T(8,128)(2,1)S(1)}, u32[]{:S(2)}, u32[]{:S(2)}) async-start(bf16[8,64,1024]{2,1,0:T(8,128)(2,1)} %bitcast.13), calls=%async_computation.3 | async-start | bytes 2097152 | tf_op jit(solution)/shard_map/all_to_all | solution.py:657
Sparse Core Ops, SparseCore 0:
  9.8 50.9 all-gather.19
  62.6 48.6 all-gather.21
  113.1 48.6 all-gather.9
  191.1 85.4 all-gather.11
  287.8 81.3 all-gather.15
  387.8 83.5 all-gather.13
  473.9 63.2 all-gather.17
